TPU v7x, 128 devices: a whole 4x4x4 slice. The times are simulated.
128 devices in a mesh: dp: 1, cpo: 2 (over core), cp: 64 (over z, y, x).
Axes of the slice: x: 4, y: 4, z: 4, core: 2. Of those that a mesh axis runs over, the one named last changes fastest.
Arguments:
- queries: bfloat16 [65536, 2, 128], P(('dp', 'cpo', 'cp'))
- keys: bfloat16 [65536, 128], P(('dp', 'cpo', 'cp'))
- values: bfloat16 [65536, 128], P(('dp', 'cpo', 'cp'))
- attn_out: bfloat16 [65536, 2, 128], P(('dp', 'cpo', 'cp'))
- logsumexp: float32 [65536, 2], P(('dp', 'cpo', 'cp'))
- d_out: bfloat16 [65536, 2, 128], P(('dp', 'cpo', 'cp'))
- cu_seqlens: int32 [174], P('dp')
Outputs:
- output 1: bfloat16 [65536, 2, 128], P(('dp', 'cpo', 'cp'))
- output 2: bfloat16 [65536, 128], P(('dp', 'cpo', 'cp'))
- output 3: bfloat16 [65536, 128], P(('dp', 'cpo', 'cp'))
All inputs are finite; a program needn't handle non-finite values.
Results may differ from a plain program's by a relative error of at most 0.00131.
Values are sent between devices in bfloat16 or wider.
A program may use at most 1 GiB of HBM per device.

v0:
```python
import jax
import jax.numpy as jnp
from jax import lax
from jax.sharding import PartitionSpec as P

HOPS = 3


def doc_ids(bounds, positions, seq_len):
    found = jnp.searchsorted(bounds[1:], positions, side="right").astype(jnp.int32)
    return jnp.where((positions >= 0) & (positions < seq_len), found, -1)


def window_backward(q_loc, do_loc, lse_loc, dot_loc, id_q, pos_q, k_win, v_win, id_k, pos_k, scale):
    rows, heads, head = q_loc.shape
    block_rows = min(64, rows)
    count = rows // block_rows
    blocks = (
        q_loc.reshape(count, block_rows, heads, head),
        do_loc.reshape(count, block_rows, heads, head),
        lse_loc.reshape(count, block_rows, heads),
        dot_loc.reshape(count, block_rows, heads),
        id_q.reshape(count, block_rows),
        pos_q.reshape(count, block_rows),
    )

    def step(carry, block):
        dk_acc, dv_acc = carry
        q_blk, do_blk, lse_blk, dot_blk, idq_blk, posq_blk = block
        keep = (idq_blk[:, None] == id_k[None, :]) & (pos_k[None, :] <= posq_blk[:, None])
        scores = jnp.einsum("qgd,kd->qgk", q_blk, k_win, preferred_element_type=jnp.float32)
        p_mat = jnp.where(keep[:, None, :], jnp.exp(scale * scores - lse_blk[:, :, None]), 0.0)
        dp_mat = jnp.einsum("qgd,kd->qgk", do_blk, v_win, preferred_element_type=jnp.float32)
        ds_mat = (p_mat * (dp_mat - dot_blk[:, :, None])).astype(jnp.bfloat16)
        dq_blk = scale * jnp.einsum("qgk,kd->qgd", ds_mat, k_win, preferred_element_type=jnp.float32)
        dk_acc = dk_acc + jnp.einsum("qgk,qgd->kd", ds_mat, q_blk, preferred_element_type=jnp.float32)
        dv_acc = dv_acc + jnp.einsum("qgk,qgd->kd", p_mat.astype(jnp.bfloat16), do_blk, preferred_element_type=jnp.float32)
        return (dk_acc, dv_acc), dq_blk.astype(jnp.bfloat16)

    width = k_win.shape[0]
    init = (jnp.zeros((width, head), jnp.float32), jnp.zeros((width, head), jnp.float32))
    (dk_sum, dv_sum), dq_blocks = lax.scan(step, init, blocks)
    return dq_blocks.reshape(rows, heads, head), dk_sum, dv_sum


def solution(mesh):
    inner = mesh.shape["cp"]
    group = mesh.shape["cpo"] * inner
    seq_axes = ("cpo", "cp")

    def local(queries, keys, values, attn_out, logsumexp, d_out, cu_seqlens):
        rows, heads, head = queries.shape
        scale = head ** -0.5
        seq_len = group * rows
        rank = lax.axis_index("cpo") * inner + lax.axis_index("cp")
        kv_pair = jnp.stack([keys, values])
        received = []
        for hop in range(HOPS, 0, -1):
            received.append(lax.ppermute(kv_pair, seq_axes, [(sender, sender + hop) for sender in range(group - hop)]))
        received.append(kv_pair)
        kv_win = jnp.concatenate(received, axis=1)
        pos_q = rank * rows + jnp.arange(rows, dtype=jnp.int32)
        pos_k = (rank - HOPS) * rows + jnp.arange((HOPS + 1) * rows, dtype=jnp.int32)
        id_q = doc_ids(cu_seqlens, pos_q, seq_len)
        id_k = doc_ids(cu_seqlens, pos_k, seq_len)
        row_dot = jnp.einsum("qgd,qgd->qg", d_out, attn_out, preferred_element_type=jnp.float32)
        d_query, dk_sum, dv_sum = window_backward(queries, d_out, logsumexp, row_dot, id_q, pos_q, kv_win[0], kv_win[1], id_k, pos_k, scale)
        part_sums = jnp.stack([dk_sum, dv_sum]).reshape(2, HOPS + 1, rows, head)
        owned = part_sums[:, HOPS]
        for hop in range(1, HOPS + 1):
            owned = owned + lax.ppermute(part_sums[:, HOPS - hop], seq_axes, [(sender, sender - hop) for sender in range(hop, group)])
        return d_query, (scale * owned[0]).astype(jnp.bfloat16), owned[1].astype(jnp.bfloat16)

    seq_spec = P(("dp", "cpo", "cp"))
    return jax.shard_map(local, mesh=mesh, in_specs=(seq_spec, seq_spec, seq_spec, seq_spec, seq_spec, seq_spec, P("dp")), out_specs=(seq_spec, seq_spec, seq_spec), check_vma=False)
```

profile of v0, /device:TPU:94, one launch (start us, length us, event | category | flops | bytes accessed | tf_op | source)
XLA Modules:
  0.0 235.5 jit_solution(4622100296219540425)
XLA Ops:
  0.6 1.0 pad_maximum_fusion.1
  1.6 3.5 %collective-permute-start = (bf16[2,512,128]{2,1,0:T(8,128)(2,1)S(1)}, bf16[2,512,128]{2,1,0:T(8,128)(2,1)S(1)}, u32[]{:S(2)}, u32[]{:S(2)}) collective-permute-start(bf16[2,512,128]{2,1,0:T(8,128)(2,1)S(1)} %pad_maximum_fusion.1), channel_id=1, source_target_pairs={{0,3},{1,4},{2,5},{3,6},{4,7},{5,8},{6,9},{7,10},{8,11},{9,12},{10... | collective-permute-start | bytes 786440 | tf_op jit(solution)/shard_map/ppermute | solution.py:59
  5.1 4.0 %collective-permute-start.1 = (bf16[2,512,128]{2,1,0:T(8,128)(2,1)S(1)}, bf16[2,512,128]{2,1,0:T(8,128)(2,1)S(1)}, u32[]{:S(2)}, u32[]{:S(2)}) collective-permute-start(bf16[2,512,128]{2,1,0:T(8,128)(2,1)S(1)} %pad_maximum_fusion.1), channel_id=1, source_target_pairs={{0,2},{1,3},{2,4},{3,5},{4,6},{5,7},{6,8},{7,9},{8,10},{9,11},{10,... | collective-permute-start | bytes 786440 | tf_op jit(solution)/shard_map/ppermute | solution.py:59
  9.1 4.0 %collective-permute-start.2 = (bf16[2,512,128]{2,1,0:T(8,128)(2,1)S(1)}, bf16[2,512,128]{2,1,0:T(8,128)(2,1)S(1)}, u32[]{:S(2)}, u32[]{:S(2)}) collective-permute-start(bf16[2,512,128]{2,1,0:T(8,128)(2,1)S(1)} %pad_maximum_fusion.1), channel_id=1, source_target_pairs={{0,1},{1,2},{2,3},{3,4},{4,5},{5,6},{6,7},{7,8},{8,9},{9,10},{10,1... | collective-permute-start | bytes 786440 | tf_op jit(solution)/shard_map/ppermute | solution.py:59
  13.2 0.8 slice.29
  13.9 105.8 %while.64 = (s32[]{:T(128)}, u32[2048]{0:T(1024)S(1)}, u32[2048]{0:T(1024)S(1)}, s32[173]{0:T(256)S(1)}, s32[]{:T(128)}, /*index=5*/s32[]{:T(128)}, s32[]{:T(128)}, s32[]{}) while((s32[]{:T(128)}, u32[2048]{0:T(1024)S(1)}, u32[2048]{0:T(1024)S(1)}, s32[173]{0:T(256)S(1)}, s32[]{:T(128)}, /*index=5*/s32[]{:T(128)}, s32[]{:T(128)}, ...), condition=%wide.region_3.4_spmd.clone, body=%wide.region_2.3_spmd.clone.sunk | while | flops 40964 | bytes 127089 | solution.py:10
  14.0 13.1 %gather_fusion.1 = s32[2048]{0:T(1024)S(1)} fusion(s32[173]{0:T(256)S(1)} %get-tuple-element.583, u32[2048]{0:T(1024)S(1)} %broadcast_clamp_fusion.2), kind=kCustom, calls=%fused_computation.1.clone.clone.1 | custom fusion | bytes 24576 | tf_op jit(solution)/shard_map/jit(searchsorted)/jit(_searchsorted_scan_impl)/vmap(jit(_searchsorted_scan_impl))/while/body/eval_jaxpr/gather | solution.py:10
  27.2 13.1 %gather_fusion.1 = s32[2048]{0:T(1024)S(1)} fusion(s32[173]{0:T(256)S(1)} %get-tuple-element.583, u32[2048]{0:T(1024)S(1)} %broadcast_clamp_fusion.2), kind=kCustom, calls=%fused_computation.1.clone.clone.1 | custom fusion | bytes 24576 | tf_op jit(solution)/shard_map/jit(searchsorted)/jit(_searchsorted_scan_impl)/vmap(jit(_searchsorted_scan_impl))/while/body/eval_jaxpr/gather | solution.py:10
  40.4 13.1 %gather_fusion.1 = s32[2048]{0:T(1024)S(1)} fusion(s32[173]{0:T(256)S(1)} %get-tuple-element.583, u32[2048]{0:T(1024)S(1)} %broadcast_clamp_fusion.2), kind=kCustom, calls=%fused_computation.1.clone.clone.1 | custom fusion | bytes 24576 | tf_op jit(solution)/shard_map/jit(searchsorted)/jit(_searchsorted_scan_impl)/vmap(jit(_searchsorted_scan_impl))/while/body/eval_jaxpr/gather | solution.py:10
  53.6 13.1 %gather_fusion.1 = s32[2048]{0:T(1024)S(1)} fusion(s32[173]{0:T(256)S(1)} %get-tuple-element.583, u32[2048]{0:T(1024)S(1)} %broadcast_clamp_fusion.2), kind=kCustom, calls=%fused_computation.1.clone.clone.1 | custom fusion | bytes 24576 | tf_op jit(solution)/shard_map/jit(searchsorted)/jit(_searchsorted_scan_impl)/vmap(jit(_searchsorted_scan_impl))/while/body/eval_jaxpr/gather | solution.py:10
  66.8 13.1 %gather_fusion.1 = s32[2048]{0:T(1024)S(1)} fusion(s32[173]{0:T(256)S(1)} %get-tuple-element.583, u32[2048]{0:T(1024)S(1)} %broadcast_clamp_fusion.2), kind=kCustom, calls=%fused_computation.1.clone.clone.1 | custom fusion | bytes 24576 | tf_op jit(solution)/shard_map/jit(searchsorted)/jit(_searchsorted_scan_impl)/vmap(jit(_searchsorted_scan_impl))/while/body/eval_jaxpr/gather | solution.py:10
  80.1 13.1 %gather_fusion.1 = s32[2048]{0:T(1024)S(1)} fusion(s32[173]{0:T(256)S(1)} %get-tuple-element.583, u32[2048]{0:T(1024)S(1)} %broadcast_clamp_fusion.2), kind=kCustom, calls=%fused_computation.1.clone.clone.1 | custom fusion | bytes 24576 | tf_op jit(solution)/shard_map/jit(searchsorted)/jit(_searchsorted_scan_impl)/vmap(jit(_searchsorted_scan_impl))/while/body/eval_jaxpr/gather | solution.py:10
  93.3 13.1 %gather_fusion.1 = s32[2048]{0:T(1024)S(1)} fusion(s32[173]{0:T(256)S(1)} %get-tuple-element.583, u32[2048]{0:T(1024)S(1)} %broadcast_clamp_fusion.2), kind=kCustom, calls=%fused_computation.1.clone.clone.1 | custom fusion | bytes 24576 | tf_op jit(solution)/shard_map/jit(searchsorted)/jit(_searchsorted_scan_impl)/vmap(jit(_searchsorted_scan_impl))/while/body/eval_jaxpr/gather | solution.py:10
  106.5 13.1 %gather_fusion.1 = s32[2048]{0:T(1024)S(1)} fusion(s32[173]{0:T(256)S(1)} %get-tuple-element.583, u32[2048]{0:T(1024)S(1)} %broadcast_clamp_fusion.2), kind=kCustom, calls=%fused_computation.1.clone.clone.1 | custom fusion | bytes 24576 | tf_op jit(solution)/shard_map/jit(searchsorted)/jit(_searchsorted_scan_impl)/vmap(jit(_searchsorted_scan_impl))/while/body/eval_jaxpr/gather | solution.py:10
  119.7 28.8 %while.63 = (s32[]{:T(128)}, u32[512]{0:T(512)S(1)}, u32[512]{0:T(512)S(1)}, s32[173]{0:T(256)S(1)}, s32[]{:T(128)}, /*index=5*/s32[]{:T(128)}, s32[]{:T(128)}, s32[]{}) while((s32[]{:T(128)}, u32[512]{0:T(512)S(1)}, u32[512]{0:T(512)S(1)}, s32[173]{0:T(256)S(1)}, s32[]{:T(128)}, /*index=5*/s32[]{:T(128)}, s32[]{:T(128)}, ...), condition=%wide.region_1.2_spmd.clone, body=%wide.region_0.1_spmd.clone.sunk | while | flops 10756 | bytes 38001 | solution.py:10
  119.8 3.5 %gather_fusion = s32[512]{0:T(512)S(1)} fusion(s32[173]{0:T(256)S(1)} %get-tuple-element.559, u32[1024]{0:T(1024)S(1)} %pad_clamp_fusion.2), kind=kCustom, calls=%fused_computation.clone.clone.1 | custom fusion | bytes 6144 | tf_op jit(solution)/shard_map/jit(searchsorted)/jit(_searchsorted_scan_impl)/vmap(jit(_searchsorted_scan_impl))/while/body/eval_jaxpr/gather | solution.py:10
  123.4 3.5 %gather_fusion = s32[512]{0:T(512)S(1)} fusion(s32[173]{0:T(256)S(1)} %get-tuple-element.559, u32[1024]{0:T(1024)S(1)} %pad_clamp_fusion.2), kind=kCustom, calls=%fused_computation.clone.clone.1 | custom fusion | bytes 6144 | tf_op jit(solution)/shard_map/jit(searchsorted)/jit(_searchsorted_scan_impl)/vmap(jit(_searchsorted_scan_impl))/while/body/eval_jaxpr/gather | solution.py:10
  127.0 3.5 %gather_fusion = s32[512]{0:T(512)S(1)} fusion(s32[173]{0:T(256)S(1)} %get-tuple-element.559, u32[1024]{0:T(1024)S(1)} %pad_clamp_fusion.2), kind=kCustom, calls=%fused_computation.clone.clone.1 | custom fusion | bytes 6144 | tf_op jit(solution)/shard_map/jit(searchsorted)/jit(_searchsorted_scan_impl)/vmap(jit(_searchsorted_scan_impl))/while/body/eval_jaxpr/gather | solution.py:10
  130.6 3.5 %gather_fusion = s32[512]{0:T(512)S(1)} fusion(s32[173]{0:T(256)S(1)} %get-tuple-element.559, u32[1024]{0:T(1024)S(1)} %pad_clamp_fusion.2), kind=kCustom, calls=%fused_computation.clone.clone.1 | custom fusion | bytes 6144 | tf_op jit(solution)/shard_map/jit(searchsorted)/jit(_searchsorted_scan_impl)/vmap(jit(_searchsorted_scan_impl))/while/body/eval_jaxpr/gather | solution.py:10
  134.2 3.5 %gather_fusion = s32[512]{0:T(512)S(1)} fusion(s32[173]{0:T(256)S(1)} %get-tuple-element.559, u32[1024]{0:T(1024)S(1)} %pad_clamp_fusion.2), kind=kCustom, calls=%fused_computation.clone.clone.1 | custom fusion | bytes 6144 | tf_op jit(solution)/shard_map/jit(searchsorted)/jit(_searchsorted_scan_impl)/vmap(jit(_searchsorted_scan_impl))/while/body/eval_jaxpr/gather | solution.py:10
  137.8 3.5 %gather_fusion = s32[512]{0:T(512)S(1)} fusion(s32[173]{0:T(256)S(1)} %get-tuple-element.559, u32[1024]{0:T(1024)S(1)} %pad_clamp_fusion.2), kind=kCustom, calls=%fused_computation.clone.clone.1 | custom fusion | bytes 6144 | tf_op jit(solution)/shard_map/jit(searchsorted)/jit(_searchsorted_scan_impl)/vmap(jit(_searchsorted_scan_impl))/while/body/eval_jaxpr/gather | solution.py:10
  141.4 3.5 %gather_fusion = s32[512]{0:T(512)S(1)} fusion(s32[173]{0:T(256)S(1)} %get-tuple-element.559, u32[1024]{0:T(1024)S(1)} %pad_clamp_fusion.2), kind=kCustom, calls=%fused_computation.clone.clone.1 | custom fusion | bytes 6144 | tf_op jit(solution)/shard_map/jit(searchsorted)/jit(_searchsorted_scan_impl)/vmap(jit(_searchsorted_scan_impl))/while/body/eval_jaxpr/gather | solution.py:10
  145.0 3.5 %gather_fusion = s32[512]{0:T(512)S(1)} fusion(s32[173]{0:T(256)S(1)} %get-tuple-element.559, u32[1024]{0:T(1024)S(1)} %pad_clamp_fusion.2), kind=kCustom, calls=%fused_computation.clone.clone.1 | custom fusion | bytes 6144 | tf_op jit(solution)/shard_map/jit(searchsorted)/jit(_searchsorted_scan_impl)/vmap(jit(_searchsorted_scan_impl))/while/body/eval_jaxpr/gather | solution.py:10
  148.6 0.6 fusion.32
  149.8 0.9 slice_bitcast_fusion
  150.6 40.8 %while.65 = (s32[]{:T(128)}, f32[2048,128]{1,0:T(8,128)S(1)}, f32[2048,128]{1,0:T(8,128)}, bf16[8,64,2,128]{3,2,1,0:T(2,128)(2,1)}, s32[8,64]{1,0:T(8,128)S(1)},...) while((s32[]{:T(128)}, f32[2048,128]{1,0:T(8,128)S(1)}, ...), condition=%wide.region_5.6_spmd.clone, body=%wide.region_4.5_spmd.clone.sunk | while | flops 338855936 | bytes 21624072 | solution.py:42
  150.8 0.8 constant_dynamic-slice_fusion.9
  152.9 0.7 copy-done
  154.4 0.7 copy-done.1
  155.1 0.6 copy_dynamic-update-slice_fusion.2
  155.9 0.8 constant_dynamic-slice_fusion.9
  158.0 0.7 copy-done
  159.5 0.7 copy-done.1
  160.2 0.6 copy_dynamic-update-slice_fusion.2
  161.0 0.8 constant_dynamic-slice_fusion.9
  163.1 0.7 copy-done
  164.6 0.7 copy-done.1
  165.3 0.6 copy_dynamic-update-slice_fusion.2
  166.2 0.8 constant_dynamic-slice_fusion.9
  168.2 0.7 copy-done
  169.7 0.7 copy-done.1
  170.4 0.6 copy_dynamic-update-slice_fusion.2
  171.3 0.8 constant_dynamic-slice_fusion.9
  173.3 0.7 copy-done
  174.8 0.7 copy-done.1
  175.5 0.6 copy_dynamic-update-slice_fusion.2
  176.4 0.8 constant_dynamic-slice_fusion.9
  178.4 0.7 copy-done
  179.9 0.7 copy-done.1
  181.5 0.8 constant_dynamic-slice_fusion.9
  183.5 0.7 copy-done
  185.0 0.7 copy-done.1
  186.6 0.8 constant_dynamic-slice_fusion.9
  188.6 0.7 copy-done
  190.1 0.7 copy-done.1
  191.5 1.3 fusion.30
  192.8 1.9 collective-permute-start.3
  194.7 3.2 %collective-permute-start.4 = (f32[2,512,128]{2,1,0:T(8,128)S(1)}, f32[2,512,128]{2,1,0:T(8,128)S(1)}, u32[]{:S(2)}, u32[]{:S(2)}) collective-permute-start(f32[2,512,128]{2,1,0:T(8,128)S(1)} %get-tuple-element.374), channel_id=1, source_target_pairs={{2,0},{3,1},{4,2},{5,3},{6,4},{7,5},{8,6},{9,7},{10,8},{11,9},{12,... | collective-permute-start | bytes 1572872 | tf_op jit(solution)/shard_map/ppermute | solution.py:71
  197.9 4.5 %collective-permute-start.5 = (f32[2,512,128]{2,1,0:T(8,128)S(1)}, f32[2,512,128]{2,1,0:T(8,128)S(1)}, u32[]{:S(2)}, u32[]{:S(2)}) collective-permute-start(f32[2,512,128]{2,1,0:T(8,128)S(1)} %get-tuple-element.373), channel_id=1, source_target_pairs={{3,0},{4,1},{5,2},{6,3},{7,4},{8,5},{9,6},{10,7},{11,8},{12,9},{13... | collective-permute-start | bytes 1572872 | tf_op jit(solution)/shard_map/ppermute | solution.py:71
  202.5 25.2 %collective-permute-done.3 = f32[2,512,128]{2,1,0:T(8,128)S(1)} collective-permute-done((f32[2,512,128]{2,1,0:T(8,128)S(1)}, f32[2,512,128]{2,1,0:T(8,128)S(1)}, u32[]{:S(2)}, u32[]{:S(2)}) %collective-permute-start.3) | collective-permute-done | bytes 524320 | tf_op jit(solution)/shard_map/ppermute | solution.py:71
  227.6 3.2 %collective-permute-done.4 = f32[2,512,128]{2,1,0:T(8,128)S(1)} collective-permute-done((f32[2,512,128]{2,1,0:T(8,128)S(1)}, f32[2,512,128]{2,1,0:T(8,128)S(1)}, u32[]{:S(2)}, u32[]{:S(2)}) %collective-permute-start.4) | collective-permute-done | bytes 524320 | tf_op jit(solution)/shard_map/ppermute | solution.py:71
  230.8 3.2 %collective-permute-done.5 = f32[2,512,128]{2,1,0:T(8,128)S(1)} collective-permute-done((f32[2,512,128]{2,1,0:T(8,128)S(1)}, f32[2,512,128]{2,1,0:T(8,128)S(1)}, u32[]{:S(2)}, u32[]{:S(2)}) %collective-permute-start.5) | collective-permute-done | bytes 524320 | tf_op jit(solution)/shard_map/ppermute | solution.py:71
  234.1 0.7 fusion.34
  234.8 0.7 fusion.35
  (217 shorter events, 20.0 us)
Async XLA Ops:
  1.6 148.0 %collective-permute-start = (bf16[2,512,128]{2,1,0:T(8,128)(2,1)S(1)}, bf16[2,512,128]{2,1,0:T(8,128)(2,1)S(1)}, u32[]{:S(2)}, u32[]{:S(2)}) collective-permute-start(bf16[2,512,128]{2,1,0:T(8,128)(2,1)S(1)} %pad_maximum_fusion.1), channel_id=1, source_target_pairs={{0,3},{1,4},{2,5},{3,6},{4,7},{5,8},{6,9},{7,10},{8,11},{9,12},{10... | collective-permute-start | bytes 786440 | tf_op jit(solution)/shard_map/ppermute | solution.py:59
  5.1 144.6 %collective-permute-start.1 = (bf16[2,512,128]{2,1,0:T(8,128)(2,1)S(1)}, bf16[2,512,128]{2,1,0:T(8,128)(2,1)S(1)}, u32[]{:S(2)}, u32[]{:S(2)}) collective-permute-start(bf16[2,512,128]{2,1,0:T(8,128)(2,1)S(1)} %pad_maximum_fusion.1), channel_id=1, source_target_pairs={{0,2},{1,3},{2,4},{3,5},{4,6},{5,7},{6,8},{7,9},{8,10},{9,11},{10,... | collective-permute-start | bytes 786440 | tf_op jit(solution)/shard_map/ppermute | solution.py:59
  9.1 140.5 %collective-permute-start.2 = (bf16[2,512,128]{2,1,0:T(8,128)(2,1)S(1)}, bf16[2,512,128]{2,1,0:T(8,128)(2,1)S(1)}, u32[]{:S(2)}, u32[]{:S(2)}) collective-permute-start(bf16[2,512,128]{2,1,0:T(8,128)(2,1)S(1)} %pad_maximum_fusion.1), channel_id=1, source_target_pairs={{0,1},{1,2},{2,3},{3,4},{4,5},{5,6},{6,7},{7,8},{8,9},{9,10},{10,1... | collective-permute-start | bytes 786440 | tf_op jit(solution)/shard_map/ppermute | solution.py:59
  119.7 28.9 %copy-start.4 = (bf16[512,2,128]{2,1,0:T(2,128)(2,1)S(1)}, bf16[512,2,128]{2,1,0:T(2,128)(2,1)}, u32[]{:S(2)}) copy-start(bf16[512,2,128]{2,1,0:T(2,128)(2,1)} %param.18) | copy-start | bytes 786436
  119.7 28.9 %copy-start.7 = (bf16[512,2,128]{2,1,0:T(2,128)(2,1)S(1)}, bf16[512,2,128]{2,1,0:T(2,128)(2,1)}, u32[]{:S(2)}) copy-start(bf16[512,2,128]{2,1,0:T(2,128)(2,1)} %param.16) | copy-start | bytes 786436
  148.6 1.0 copy-start.8
  148.6 1.1 copy-start.5
  148.6 1.1 copy-start.6
  150.6 1.4 copy-start.3
  152.4 1.2 copy-start
  154.1 1.0 copy-start.1
  155.8 1.4 copy-start.3
  157.5 1.2 copy-start
  159.2 1.0 copy-start.1
  160.9 1.4 copy-start.3
  162.6 1.2 copy-start
  164.3 1.0 copy-start.1
  166.0 1.4 copy-start.3
  167.7 1.2 copy-start
  169.4 1.0 copy-start.1
  171.1 1.4 copy-start.3
  172.8 1.2 copy-start
  174.5 1.0 copy-start.1
  176.2 1.4 copy-start.3
  177.9 1.2 copy-start
  179.6 1.0 copy-start.1
  181.3 1.4 copy-start.3
  183.0 1.2 copy-start
  184.7 1.0 copy-start.1
  186.4 1.4 copy-start.3
  188.1 1.2 copy-start
  189.8 1.0 copy-start.1
  191.5 42.5 %copy-start.2 = (f32[2048,128]{1,0:T(8,128)S(1)}, f32[2048,128]{1,0:T(8,128)}, u32[]{:S(2)}) copy-start(f32[2048,128]{1,0:T(8,128)} %get-tuple-element.211) | copy-start | bytes 3145732
  192.8 34.9 %collective-permute-start.3 = (f32[2,512,128]{2,1,0:T(8,128)S(1)}, f32[2,512,128]{2,1,0:T(8,128)S(1)}, u32[]{:S(2)}, u32[]{:S(2)}) collective-permute-start(f32[2,512,128]{2,1,0:T(8,128)S(1)} %get-tuple-element.372), channel_id=1, source_target_pairs={{1,0},{2,1},{3,2},{4,3},{5,4},{6,5},{7,6},{8,7},{9,8},{10,9},{11,1... | collective-permute-start | bytes 1572872 | tf_op jit(solution)/shard_map/ppermute | solution.py:71
  194.7 36.1 %collective-permute-start.4 = (f32[2,512,128]{2,1,0:T(8,128)S(1)}, f32[2,512,128]{2,1,0:T(8,128)S(1)}, u32[]{:S(2)}, u32[]{:S(2)}) collective-permute-start(f32[2,512,128]{2,1,0:T(8,128)S(1)} %get-tuple-element.374), channel_id=1, source_target_pairs={{2,0},{3,1},{4,2},{5,3},{6,4},{7,5},{8,6},{9,7},{10,8},{11,9},{12,... | collective-permute-start | bytes 1572872 | tf_op jit(solution)/shard_map/ppermute | solution.py:71
  197.9 36.1 %collective-permute-start.5 = (f32[2,512,128]{2,1,0:T(8,128)S(1)}, f32[2,512,128]{2,1,0:T(8,128)S(1)}, u32[]{:S(2)}, u32[]{:S(2)}) collective-permute-start(f32[2,512,128]{2,1,0:T(8,128)S(1)} %get-tuple-element.373), channel_id=1, source_target_pairs={{3,0},{4,1},{5,2},{6,3},{7,4},{8,5},{9,6},{10,7},{11,8},{12,9},{13... | collective-permute-start | bytes 1572872 | tf_op jit(solution)/shard_map/ppermute | solution.py:71
where the time goes:
time: 236 us; the launch traced here: 235 us
  local copies, waits for them, and re-layouts  159 us (67%)
  waiting for transfers between devices  31.6 us (13%)
  starting transfers between devices  21.2 us (9%)
  matrix products  15.2 us (6%)
  other arithmetic  5.79 us (2%)
    gather x16, local copies, waits for them, and re-layouts, doc_ids(): jnp.searchsorted(bounds[1:], positions, side='right').astype(jnp.int32)  133 us
    ppermute x3, waiting for transfers between devices, local(): lax.ppermute(part_sums[:, HOPS - hop], seq_axes, [(sender, sender - hop)...  31.6 us
    while x64, local copies, waits for them, and re-layouts  11.5 us
    ppermute x3, starting transfers between devices, local(): lax.ppermute(kv_pair, seq_axes, [(sender, sender + hop) for sender in ran...  11.5 us
    ppermute x3, starting transfers between devices, local(): lax.ppermute(part_sums[:, HOPS - hop], seq_axes, [(sender, sender - hop)...  9.66 us
    dynamic_slice x16, local copies, waits for them, and re-layouts, window_backward(): (dk_sum, dv_sum), dq_blocks = lax.scan(step, init, blocks)  6.58 us
    dynamic_update_slice x8, local copies, waits for them, and re-layouts, window_backward(): (dk_sum, dv_sum), dq_blocks = lax.scan(step, init, blocks)  5.19 us
  transfers between devices with their start and end apart: 6, of which 3 were waited for; matrix products, arithmetic and copies ran while one was open for 58% of the time, Pallas kernels for 0%

commit v1 on v0

v1 whole, which is shorter than its diff:
```python
import functools
import math

import jax
import jax.numpy as jnp
from jax import lax
from jax.experimental import pallas as pl
from jax.experimental.pallas import tpu as pltpu
from jax.sharding import PartitionSpec as P

MESH = pl.DeviceIdType.MESH
HOPS = 3
CHUNKS = 4
LOG2E = math.log2(math.e)
NT = (((1,), (1,)), ((), ()))
NN = (((1,), (0,)), ((), ()))


def dot(lhs, rhs, dims):
    return lax.dot_general(lhs, rhs, dims, preferred_element_type=jnp.float32)


def backward_kernel(sizes, q_hbm, k_hbm, v_hbm, o_hbm, do_hbm, lse_ref, cu_ref, dq_hbm, dk_hbm, dv_hbm,
                    kv_own, kv_in, qd_own, qd_in, o_buf, ld_own, ld_in, starts, key_t, dq_t, dk_acc, dv_acc,
                    dq_buf, dk_buf, dv_buf, load_sem, store_sem,
                    kv_send, kv_recv, qd_send, qd_recv, ld_send, ld_recv):
    outer, inner, rows, heads, head = sizes
    group = outer * inner
    scale = head ** -0.5
    span = rows // CHUNKS
    lanes = span * heads
    bounds = cu_ref.shape[1]
    rank = lax.axis_index("cpo") * inner + lax.axis_index("cp")

    def device(index):
        return (0, index // inner, index % inner)

    right = device((rank + 1) % group)
    left = device((rank + group - 1) % group)

    loads = [
        pltpu.make_async_copy(k_hbm, kv_own.at[0], load_sem.at[0]),
        pltpu.make_async_copy(v_hbm, kv_own.at[1], load_sem.at[1]),
        pltpu.make_async_copy(q_hbm, qd_own.at[0], load_sem.at[2]),
        pltpu.make_async_copy(do_hbm, qd_own.at[1], load_sem.at[3]),
        pltpu.make_async_copy(o_hbm, o_buf, load_sem.at[4]),
    ]
    for load in loads:
        load.start()

    barrier = pltpu.get_barrier_semaphore()
    for peer in (left, right):
        pl.semaphore_signal(barrier, inc=1, device_id=peer, device_id_type=MESH)
    pl.semaphore_wait(barrier, 2)

    def kv_copy(hop, chunk):
        source = kv_own if hop == 0 else kv_in.at[hop - 1]
        part = pl.ds(chunk * span, span)
        return pltpu.make_async_remote_copy(
            src_ref=source.at[:, part], dst_ref=kv_in.at[hop, :, part],
            send_sem=kv_send.at[hop, chunk], recv_sem=kv_recv.at[hop, chunk],
            device_id=right, device_id_type=MESH)

    def qd_copy(hop, chunk):
        source = qd_own if hop == 0 else qd_in.at[hop - 1]
        part = pl.ds(chunk * lanes, lanes)
        return pltpu.make_async_remote_copy(
            src_ref=source.at[:, part], dst_ref=qd_in.at[hop, :, part],
            send_sem=qd_send.at[hop, chunk], recv_sem=qd_recv.at[hop, chunk],
            device_id=left, device_id_type=MESH)

    def ld_copy(hop):
        source = ld_own if hop == 0 else ld_in.at[hop - 1]
        return pltpu.make_async_remote_copy(
            src_ref=source, dst_ref=ld_in.at[hop],
            send_sem=ld_send.at[hop], recv_sem=ld_recv.at[hop],
            device_id=left, device_id_type=MESH)

    loads[0].wait()
    loads[1].wait()
    for chunk in range(CHUNKS):
        kv_copy(0, chunk).start()
    loads[2].wait()
    loads[3].wait()
    for chunk in range(CHUNKS):
        qd_copy(0, chunk).start()
    loads[4].wait()

    ld_own[0:1, :] = lse_ref[...] * LOG2E
    for part in range(rows * heads // head):
        piece = slice(part * head, (part + 1) * head)
        prod = qd_own[1, piece, :].astype(jnp.float32) * o_buf[piece, :].astype(jnp.float32)
        ld_own[1:2, piece] = jnp.sum(prod.T, axis=0, keepdims=True)

    first = (rank * rows).astype(jnp.float32)
    cuts = cu_ref[...].astype(jnp.float32)
    padded = -(-bounds // head) * head
    cut_cols = []
    for base in range(0, padded, head):
        width = min(head, bounds - base)
        row = cuts[:, base:base + width]
        if width < head:
            row = jnp.concatenate([row, jnp.zeros((1, head - width), jnp.float32)], axis=1)
        cut_cols.append(jnp.broadcast_to(row, (head, head)).T - first)
    lane = lax.broadcasted_iota(jnp.int32, (1, head), 1)

    def fill_starts(step, _):
        lane_base = pl.multiple_of((step % (rows * heads // head)) * head, head)
        hop = step // (rows * heads // head)
        token = ((lane + lane_base) // heads + hop * rows).astype(jnp.float32)
        best = jnp.full((head, head), -1e9, jnp.float32)
        for col in cut_cols:
            best = jnp.maximum(best, jnp.where(col <= token, col, -1e9))
        starts[hop, :, pl.ds(lane_base, head)] = jnp.max(best, axis=0, keepdims=True)
        return 0

    lax.fori_loop(0, (HOPS + 1) * rows * heads // head, fill_starts, 0)

    dk_acc[...] = jnp.zeros_like(dk_acc)
    dv_acc[...] = jnp.zeros_like(dv_acc)
    dq_t[...] = jnp.zeros_like(dq_t)

    def tile(kv, k_from, k_to, qd, ld, chunk, key_shift, start_slot, q_side, k_side):
        part = slice(chunk * lanes, (chunk + 1) * lanes)
        key_rows = slice(k_from, k_to)
        keys, vals = kv[0, key_rows, :], kv[1, key_rows, :]
        qry, dout = qd[0, part, :], qd[1, part, :]
        score = dot(keys, qry, NT)
        grad = dot(vals, dout, NT)
        lse, row_dot = ld[0:1, part], ld[1:2, part]
        start = starts[start_slot, :, part]
        key_pos = lax.broadcasted_iota(jnp.int32, (k_to - k_from, lanes), 0).astype(jnp.float32)
        keep = key_pos >= start - float(key_shift * rows + k_from)
        if q_side and k_side:
            token = lax.broadcasted_iota(jnp.int32, (1, lanes), 1) // heads + (chunk * span - k_from)
            keep = keep & (key_pos <= token.astype(jnp.float32))
        prob = jnp.where(keep, jnp.exp2(score * (scale * LOG2E) - lse), 0.0)
        dsc = (prob * (grad - row_dot)).astype(jnp.bfloat16)
        if k_side:
            dv_acc[key_rows, :] += dot(prob.astype(jnp.bfloat16), dout, NN)
            dk_acc[key_rows, :] += dot(dsc, qry, NN)
        if q_side:
            dq_t[:, part] += dot(key_t[:, key_rows], dsc, NN)

    key_t[...] = kv_own[0].T
    for chunk in range(CHUNKS):
        tile(kv_own, 0, (chunk + 1) * span, qd_own, ld_own, chunk, 0, 0, True, True)
    ld_copy(0).start()

    def keys_ready(hop):
        key_t[...] = kv_in[hop - 1, 0].T
        for chunk in range(CHUNKS):
            k_from = chunk * span if hop == HOPS else 0
            tile(kv_in.at[hop - 1], k_from, rows, qd_own, ld_own, chunk, -hop, 0, True, False)

    for step in range(HOPS * CHUNKS):
        for index in (2 * step, 2 * step + 1):
            if index < HOPS * CHUNKS:
                hop, chunk = index // CHUNKS, index % CHUNKS
                kv_copy(hop, chunk).wait_recv()
                if hop + 1 < HOPS:
                    kv_copy(hop + 1, chunk).start()
        hop, chunk = step // CHUNKS, step % CHUNKS
        if chunk == 0:
            ld_copy(hop).wait_recv()
            if hop + 1 < HOPS:
                ld_copy(hop + 1).start()
        qd_copy(hop, chunk).wait_recv()
        if hop + 1 < HOPS:
            qd_copy(hop + 1, chunk).start()
        k_from = chunk * span if hop + 1 == HOPS else 0
        tile(kv_own, k_from, rows, qd_in.at[hop], ld_in.at[hop], chunk, 0, hop + 1, False, True)
        if step % 2 == 1 and step // 2 < HOPS:
            keys_ready(step // 2 + 1)
        if step == 2 * HOPS - 1:
            for part in range(rows * heads // head):
                piece = slice(part * head, (part + 1) * head)
                dq_buf[piece, :] = (scale * dq_t[:, piece].T).astype(jnp.bfloat16)
            pltpu.make_async_copy(dq_buf, dq_hbm, store_sem.at[0]).start()

    dk_buf[...] = (scale * dk_acc[...]).astype(jnp.bfloat16)
    dv_buf[...] = dv_acc[...].astype(jnp.bfloat16)
    pltpu.make_async_copy(dk_buf, dk_hbm, store_sem.at[1]).start()
    pltpu.make_async_copy(dv_buf, dv_hbm, store_sem.at[2]).start()
    for hop in range(HOPS):
        for chunk in range(CHUNKS):
            kv_copy(hop, chunk).wait_send()
            qd_copy(hop, chunk).wait_send()
        ld_copy(hop).wait_send()
    pltpu.make_async_copy(dq_buf, dq_hbm, store_sem.at[0]).wait()
    pltpu.make_async_copy(dk_buf, dk_hbm, store_sem.at[1]).wait()
    pltpu.make_async_copy(dv_buf, dv_hbm, store_sem.at[2]).wait()


def solution(mesh):
    outer, inner = mesh.shape["cpo"], mesh.shape["cp"]

    def local(queries, keys, values, attn_out, logsumexp, d_out, cu_seqlens):
        rows, heads, head = queries.shape
        flat = rows * heads
        low, full = jnp.bfloat16, jnp.float32
        any_spec = pl.BlockSpec(memory_space=pl.ANY)
        vmem_spec = pl.BlockSpec(memory_space=pltpu.VMEM)
        dma = pltpu.SemaphoreType.DMA
        d_query, d_key, d_value = pl.pallas_call(
            functools.partial(backward_kernel, (outer, inner, rows, heads, head)),
            out_shape=(jax.ShapeDtypeStruct((flat, head), low), jax.ShapeDtypeStruct((rows, head), low), jax.ShapeDtypeStruct((rows, head), low)),
            in_specs=[any_spec] * 5 + [vmem_spec] * 2,
            out_specs=(any_spec,) * 3,
            scratch_shapes=[
                pltpu.VMEM((2, rows, head), low), pltpu.VMEM((HOPS, 2, rows, head), low),
                pltpu.VMEM((2, flat, head), low), pltpu.VMEM((HOPS, 2, flat, head), low),
                pltpu.VMEM((flat, head), low),
                pltpu.VMEM((2, flat), full), pltpu.VMEM((HOPS, 2, flat), full),
                pltpu.VMEM((HOPS + 1, 1, flat), full),
                pltpu.VMEM((head, rows), low), pltpu.VMEM((head, flat), full),
                pltpu.VMEM((rows, head), full), pltpu.VMEM((rows, head), full),
                pltpu.VMEM((flat, head), low), pltpu.VMEM((rows, head), low), pltpu.VMEM((rows, head), low),
                dma((5,)), dma((3,)),
                dma((HOPS, CHUNKS)), dma((HOPS, CHUNKS)), dma((HOPS, CHUNKS)), dma((HOPS, CHUNKS)), dma((HOPS,)), dma((HOPS,)),
            ],
            compiler_params=pltpu.CompilerParams(collective_id=0, has_side_effects=True),
        )(queries.reshape(flat, head), keys, values, attn_out.reshape(flat, head), d_out.reshape(flat, head),
          logsumexp.reshape(1, flat), cu_seqlens.reshape(1, -1))
        return d_query.reshape(rows, heads, head), d_key, d_value

    seq_spec = P(("dp", "cpo", "cp"))
    return jax.shard_map(local, mesh=mesh, in_specs=(seq_spec,) * 6 + (P("dp"),), out_specs=(seq_spec,) * 3, check_vma=False)
```

time: 236 us -> 56.5 us (0.24)
  the two profiles are of different devices: /device:TPU:94 before, /device:TPU:1 now
where the time goes in v1:
time: 56.5 us; the launch traced here: 56.3 us
  Pallas kernels  50.6 us (90%)
  local copies, waits for them, and re-layouts  5.08 us (9%)
  between operations  0.67 us (1%)
    pallas_call x1, Pallas kernels, local(): pl.pallas_call(functools.partial(backward_kernel, (outer, inner, rows, he...  50.6 us
    unnamed x10, local copies, waits for them, and re-layouts  4.3 us

profile of v1, /device:TPU:1, one launch (start us, length us, event | category | flops | bytes accessed | tf_op | source)
XLA Modules:
  0.0 56.3 jit_solution(6676413463188375892)
XLA Ops:
  0.6 0.0 copy-start.2
  0.6 0.7 %copy-done.2 = f32[512,2]{0,1:T(2,128)S(1)} copy-done((f32[512,2]{0,1:T(2,128)S(1)}, f32[512,2]{0,1:T(2,128)}, u32[]{:S(2)}) %copy-start.2) | copy-done | bytes 4120
  1.3 0.1 copy.11
  1.5 0.8 %reshape.27.lse_ref = f32[1,1024]{1,0:T(1,128)} reshape(f32[512,2]{1,0:T(8,128)S(1)} %copy.11) | data formatting | bytes 8192 | tf_op jit(solution)/shard_map/reshape | solution.py:224
  2.2 50.6 %shard_map.94 = (bf16[1024,128]{1,0:T(8,128)(2,1)}, bf16[512,128]{1,0:T(8,128)(2,1)}, bf16[512,128]{1,0:T(8,128)(2,1)}) custom-call(bf16[1024,128]{1,0:T(8,128)(2,1)} %bitcast.5, bf16[512,128]{1,0:T(8,128)(2,1)} %k_hbm.1, bf16[512,128]{1,0:T(8,128)(2,1)} %v_hbm.1, bf16[1024,128]{1,0:T(8,128)(2,1)} %bitcast.6, bf16[1024,128]{1,0:T(8,128)(2,1)} %bitcast.7, ...), custom_call_target="tpu_custom_call" | custom-call | tf_op jit(solution)/shard_map/pallas_call | solution.py:205
  52.8 0.0 copy-start.1
  52.9 1.9 %copy.15 = bf16[512,2,128]{2,1,0:T(2,128)(2,1)} copy(bf16[512,2,128]{2,1,0:T(2,128)(2,1)} %bitcast.8) | data formatting | bytes 524288
  54.7 0.0 copy-done.1
  54.7 0.0 copy-start
  54.7 0.7 %copy.16 = bf16[512,128]{1,0:T(8,128)(2,1)} copy(bf16[512,128]{1,0:T(8,128)(2,1)S(1)} %copy-done.1) | data formatting | bytes 262144
  55.4 0.3 copy-done
  55.7 0.7 %copy.17 = bf16[512,128]{1,0:T(8,128)(2,1)} copy(bf16[512,128]{1,0:T(8,128)(2,1)S(1)} %copy-done) | data formatting | bytes 262144
Async XLA Ops:
  0.6 0.7 %copy-start.2 = (f32[512,2]{0,1:T(2,128)S(1)}, f32[512,2]{0,1:T(2,128)}, u32[]{:S(2)}) copy-start(f32[512,2]{0,1:T(2,128)} %param.11) | copy-start | bytes 12292
  52.8 1.9 %copy-start.1 = (bf16[512,128]{1,0:T(8,128)(2,1)S(1)}, bf16[512,128]{1,0:T(8,128)(2,1)}, u32[]{:S(2)}) copy-start(bf16[512,128]{1,0:T(8,128)(2,1)} %get-tuple-element.13) | copy-start | bytes 393220
  54.7 1.0 %copy-start = (bf16[512,128]{1,0:T(8,128)(2,1)S(1)}, bf16[512,128]{1,0:T(8,128)(2,1)}, u32[]{:S(2)}) copy-start(bf16[512,128]{1,0:T(8,128)(2,1)} %get-tuple-element.14) | copy-start | bytes 393220

commit v2 on v1

v2 whole, which is shorter than its diff:
```python
import functools
import math

import jax
import jax.numpy as jnp
from jax import lax
from jax.experimental import pallas as pl
from jax.experimental.pallas import tpu as pltpu
from jax.sharding import PartitionSpec as P

MESH = pl.DeviceIdType.MESH
HOPS = 3
CHUNKS = 4
FAR = (1, 2, 3)
VIA = 2
LOG2E = math.log2(math.e)
NT = (((1,), (1,)), ((), ()))
NN = (((1,), (0,)), ((), ()))


def dot(lhs, rhs, dims):
    return lax.dot_general(lhs, rhs, dims, preferred_element_type=jnp.float32)


def backward_kernel(sizes, q_hbm, k_hbm, v_hbm, o_hbm, do_hbm, lse_hbm, cu_hbm, dq_out, dk_out, dv_out,
                    kv_own, kv_in, qd_own, qd_in, qd_via, o_buf, ld_own, ld_in, lse_buf, cu_buf, starts, key_t, dq_t, dk_acc, dv_acc,
                    load_sem, kv_send, kv_recv, qd_send, qd_recv, far_send, far_recv, via_recv, ld_send, ld_recv):
    outer, inner, rows, heads, head, ring = sizes
    group = outer * inner
    scale = head ** -0.5
    span = rows // CHUNKS
    lanes = span * heads
    flat = rows * heads
    bounds = cu_buf.shape[1]
    rank = lax.axis_index("cpo") * inner + lax.axis_index("cp")
    column = rank % ring

    def device(index):
        return (0, index // inner, index % inner)

    loads = [
        pltpu.make_async_copy(k_hbm, kv_own.at[0], load_sem.at[0]),
        pltpu.make_async_copy(v_hbm, kv_own.at[1], load_sem.at[1]),
        pltpu.make_async_copy(q_hbm, qd_own.at[0], load_sem.at[2]),
        pltpu.make_async_copy(do_hbm, qd_own.at[1], load_sem.at[3]),
        pltpu.make_async_copy(o_hbm, o_buf, load_sem.at[4]),
        pltpu.make_async_copy(lse_hbm, lse_buf, load_sem.at[5]),
        pltpu.make_async_copy(cu_hbm, cu_buf, load_sem.at[6]),
    ]
    for load in loads:
        load.start()

    barrier = pltpu.get_barrier_semaphore()
    arrivals = 0
    for step in (-4, -3, -1, 1, 3, 4):
        peer = rank + step
        known = (peer >= 0) & (peer < group)

        @pl.when(known)
        def _():
            pl.semaphore_signal(barrier, inc=1, device_id=device(peer), device_id_type=MESH)

        arrivals = arrivals + jnp.where(known, 1, 0)
    pl.semaphore_wait(barrier, arrivals)

    def kv_copy(hop, chunk):
        source = kv_own if hop == 0 else kv_in.at[hop - 1]
        part = pl.ds(chunk * span, span)
        return pltpu.make_async_remote_copy(
            src_ref=source.at[:, part], dst_ref=kv_in.at[hop, :, part],
            send_sem=kv_send.at[hop, chunk], recv_sem=kv_recv.at[hop, chunk],
            device_id=device(rank + 1), device_id_type=MESH)

    def qd_copy(hop, chunk):
        source = qd_own if hop == 0 else qd_in.at[hop - 1]
        part = pl.ds(chunk * lanes, lanes)
        return pltpu.make_async_remote_copy(
            src_ref=source.at[:, part], dst_ref=qd_in.at[hop, :, part],
            send_sem=qd_send.at[hop, chunk], recv_sem=qd_recv.at[hop, chunk],
            device_id=device(rank - 1), device_id_type=MESH)

    def ld_copy(hop):
        source = ld_own if hop == 0 else ld_in.at[hop - 1]
        return pltpu.make_async_remote_copy(
            src_ref=source, dst_ref=ld_in.at[hop],
            send_sem=ld_send.at[hop], recv_sem=ld_recv.at[hop],
            device_id=device(rank - 1), device_id_type=MESH)

    def far_copy(chunk):
        part = pl.ds(chunk * lanes, lanes)
        return pltpu.make_async_remote_copy(
            src_ref=qd_own.at[:, part], dst_ref=qd_in.at[HOPS - 1, :, part],
            send_sem=far_send.at[chunk], recv_sem=far_recv.at[chunk],
            device_id=device(rank - 3), device_id_type=MESH)

    def via_copy(chunk):
        part = pl.ds(chunk * lanes, lanes)
        return pltpu.make_async_remote_copy(
            src_ref=qd_own.at[:, part], dst_ref=qd_via.at[:, part],
            send_sem=far_send.at[chunk], recv_sem=via_recv.at[chunk],
            device_id=device(rank - 4), device_id_type=MESH)

    def pass_copy(chunk):
        part = pl.ds(chunk * lanes, lanes)
        return pltpu.make_async_remote_copy(
            src_ref=qd_via.at[:, part], dst_ref=qd_in.at[HOPS - 1, :, part],
            send_sem=qd_send.at[HOPS - 1, chunk], recv_sem=far_recv.at[chunk],
            device_id=device(rank + 1), device_id_type=MESH)

    sends_kv = [(rank >= hop) & (rank + 1 < group) for hop in range(HOPS)]
    gets_kv = [rank >= hop + 1 for hop in range(HOPS)]
    sends_qd = [(rank >= 1) & (rank + hop < group) for hop in range(HOPS)]
    gets_qd = [rank + hop + 1 < group for hop in range(HOPS)]
    is_via = column == VIA
    sends_far = (rank >= HOPS) & ~is_via
    sends_via = (rank >= HOPS + 1) & is_via
    passes = is_via & (rank + HOPS + 1 < group)

    loads[0].wait()
    loads[1].wait()

    @pl.when(sends_kv[0])
    def _():
        for chunk in range(CHUNKS):
            kv_copy(0, chunk).start()

    loads[2].wait()
    loads[3].wait()

    @pl.when(sends_qd[0])
    def _():
        qd_copy(0, 0).start()

    @pl.when(sends_via)
    def _():
        for chunk in FAR:
            via_copy(chunk).start()

    loads[4].wait()
    loads[5].wait()
    loads[6].wait()

    row_id = lax.broadcasted_iota(jnp.int32, (head, heads * head), 0)
    lane_id = lax.broadcasted_iota(jnp.int32, (head, heads * head), 1)
    for part in range(rows // head):
        piece = slice(part * head, (part + 1) * head)
        wide = jnp.zeros((head, heads * head), jnp.float32)
        for g in range(heads):
            column_g = jnp.broadcast_to(lse_buf[g:g + 1, piece], (head, head)).T
            wide = jnp.where(lane_id == row_id * heads + g, jnp.concatenate([column_g] * heads, axis=1), wide)
        ld_own[0:1, part * heads * head:(part + 1) * heads * head] = jnp.sum(wide, axis=0, keepdims=True) * LOG2E
    for part in range(flat // head):
        piece = slice(part * head, (part + 1) * head)
        prod = qd_own[1, piece, :].astype(jnp.float32) * o_buf[piece, :].astype(jnp.float32)
        ld_own[1:2, piece] = jnp.sum(prod.T, axis=0, keepdims=True)

    first = (rank * rows).astype(jnp.float32)
    cuts = cu_buf[...].astype(jnp.float32)
    cut_cols = []
    for base in range(0, bounds, head):
        width = min(head, bounds - base)
        row = cuts[:, base:base + width]
        if width < head:
            row = jnp.concatenate([row, jnp.zeros((1, head - width), jnp.float32)], axis=1)
        cut_cols.append(jnp.broadcast_to(row, (head, head)).T - first)
    lane = lax.broadcasted_iota(jnp.int32, (1, head), 1)

    def fill_starts(step, _):
        lane_base = pl.multiple_of((step % (flat // head)) * head, head)
        hop = step // (flat // head)
        token = ((lane + lane_base) // heads + hop * rows).astype(jnp.float32)
        best = jnp.full((head, head), -1e9, jnp.float32)
        for col in cut_cols:
            best = jnp.maximum(best, jnp.where(col <= token, col, -1e9))
        starts[hop, :, pl.ds(lane_base, head)] = jnp.max(best, axis=0, keepdims=True)
        return 0

    lax.fori_loop(0, (HOPS + 1) * flat // head, fill_starts, 0)

    @pl.when(sends_qd[0])
    def _():
        ld_copy(0).start()
        for chunk in range(1, CHUNKS):
            qd_copy(0, chunk).start()

    dk_acc[...] = jnp.zeros_like(dk_acc)
    dv_acc[...] = jnp.zeros_like(dv_acc)
    dq_t[...] = jnp.zeros_like(dq_t)

    def tile(kv, k_from, k_to, qd, ld, chunk, key_shift, start_slot, q_side, k_side):
        part = slice(chunk * lanes, (chunk + 1) * lanes)
        key_rows = slice(k_from, k_to)
        keys, vals = kv[0, key_rows, :], kv[1, key_rows, :]
        qry, dout = qd[0, part, :], qd[1, part, :]
        score = dot(keys, qry, NT)
        grad = dot(vals, dout, NT)
        lse, row_dot = ld[0:1, part], ld[1:2, part]
        start = starts[start_slot, :, part]
        key_pos = lax.broadcasted_iota(jnp.int32, (k_to - k_from, lanes), 0).astype(jnp.float32)
        keep = key_pos >= start - float(key_shift * rows + k_from)
        if q_side and k_side:
            token = lax.broadcasted_iota(jnp.int32, (1, lanes), 1) // heads + (chunk * span - k_from)
            keep = keep & (key_pos <= token.astype(jnp.float32))
        prob = jnp.where(keep, jnp.exp2(score * (scale * LOG2E) - lse), 0.0)
        dsc = (prob * (grad - row_dot)).astype(jnp.bfloat16)
        if k_side:
            dv_acc[key_rows, :] += dot(prob.astype(jnp.bfloat16), dout, NN)
            dk_acc[key_rows, :] += dot(dsc, qry, NN)
        if q_side:
            dq_t[:, part] += dot(key_t[:, key_rows], dsc, NN)

    key_t[...] = kv_own[0].T
    for chunk in range(CHUNKS):
        tile(kv_own, 0, (chunk + 1) * span, qd_own, ld_own, chunk, 0, 0, True, True)

    def keys_arrive(hop, chunks):
        @pl.when(gets_kv[hop])
        def _():
            for chunk in chunks:
                kv_copy(hop, chunk).wait_recv()

        if hop + 1 < HOPS:
            @pl.when(sends_kv[hop + 1])
            def _():
                for chunk in chunks:
                    kv_copy(hop + 1, chunk).start()

    def keys_used(hop):
        @pl.when(gets_kv[hop])
        def _():
            key_t[...] = kv_in[hop, 0].T
            for chunk in range(CHUNKS):
                k_from = chunk * span if hop + 1 == HOPS else 0
                tile(kv_in.at[hop], k_from, rows, qd_own, ld_own, chunk, -hop - 1, 0, True, False)

    def queries_arrive(hop, chunk):
        @pl.when(gets_qd[hop])
        def _():
            if hop + 1 == HOPS and chunk in FAR:
                far_copy(chunk).wait_recv()
            else:
                qd_copy(hop, chunk).wait_recv()

        if hop + 1 < HOPS and not (hop + 2 == HOPS and chunk in FAR):
            @pl.when(sends_qd[hop + 1])
            def _():
                qd_copy(hop + 1, chunk).start()

    def stats_arrive(hop):
        @pl.when(gets_qd[hop])
        def _():
            ld_copy(hop).wait_recv()

        if hop + 1 < HOPS:
            @pl.when(sends_qd[hop + 1])
            def _():
                ld_copy(hop + 1).start()

    def queries_used(hop, chunk):
        @pl.when(gets_qd[hop])
        def _():
            k_from = chunk * span if hop + 1 == HOPS else 0
            tile(kv_own, k_from, rows, qd_in.at[hop], ld_in.at[hop], chunk, 0, hop + 1, False, True)

    for slot in range(2 * CHUNKS):
        if slot < HOPS * CHUNKS // 2:
            keys_arrive(slot // 2, (2 * (slot % 2), 2 * (slot % 2) + 1))
        hop, chunk = slot // CHUNKS, slot % CHUNKS
        queries_arrive(hop, chunk)
        if chunk == 0:
            stats_arrive(hop)
        if slot == CHUNKS - 1:
            @pl.when(sends_far)
            def _():
                for far in FAR:
                    far_copy(far).start()

            @pl.when(passes)
            def _():
                for far in FAR:
                    via_copy(far).wait_recv()
                    pass_copy(far).start()
        queries_used(hop, chunk)
        if slot % 2 == 1 and slot // 2 < HOPS:
            keys_used(slot // 2)
        if slot == 2 * HOPS - 1:
            for part in range(flat // head):
                piece = slice(part * head, (part + 1) * head)
                dq_out[piece, :] = (scale * dq_t[:, piece].T).astype(jnp.bfloat16)
        if slot == 2 * HOPS - 1:
            stats_arrive(HOPS - 1)
        if slot >= 2 * HOPS:
            far = FAR[slot - 2 * HOPS]
            queries_arrive(HOPS - 1, far)
            queries_used(HOPS - 1, far)
    rest = [chunk for chunk in range(CHUNKS) if chunk not in FAR]
    for chunk in rest + list(FAR[2 * CHUNKS - 2 * HOPS:]):
        queries_arrive(HOPS - 1, chunk)
        queries_used(HOPS - 1, chunk)

    dk_out[...] = (scale * dk_acc[...]).astype(jnp.bfloat16)
    dv_out[...] = dv_acc[...].astype(jnp.bfloat16)
    for hop in range(HOPS):
        @pl.when(sends_kv[hop])
        def _():
            for chunk in range(CHUNKS):
                kv_copy(hop, chunk).wait_send()

        @pl.when(sends_qd[hop])
        def _():
            for chunk in range(CHUNKS) if hop + 1 < HOPS else rest:
                qd_copy(hop, chunk).wait_send()
            ld_copy(hop).wait_send()

    @pl.when(sends_far | sends_via)
    def _():
        for chunk in FAR:
            far_copy(chunk).wait_send()

    @pl.when(passes)
    def _():
        for chunk in FAR:
            pass_copy(chunk).wait_send()


def store_kernel(dq_in, dk_in, dv_in, dq_hbm, dk_hbm, dv_hbm, sem):
    copies = [pltpu.make_async_copy(source, target, sem.at[index])
              for index, (source, target) in enumerate(((dq_in, dq_hbm), (dk_in, dk_hbm), (dv_in, dv_hbm)))]
    for copy in copies:
        copy.start()
    for copy in copies:
        copy.wait()


def solution(mesh):
    outer, inner = mesh.shape["cpo"], mesh.shape["cp"]
    ring = round(inner ** (1 / 3))

    def local(queries, keys, values, attn_out, logsumexp, d_out, cu_seqlens):
        rows, heads, head = queries.shape
        flat = rows * heads
        low, full = jnp.bfloat16, jnp.float32
        any_spec = pl.BlockSpec(memory_space=pl.ANY)
        vmem_spec = pl.BlockSpec(memory_space=pltpu.VMEM)
        dma = pltpu.SemaphoreType.DMA
        shapes = (jax.ShapeDtypeStruct((flat, head), low), jax.ShapeDtypeStruct((rows, head), low), jax.ShapeDtypeStruct((rows, head), low))
        grads = pl.pallas_call(
            functools.partial(backward_kernel, (outer, inner, rows, heads, head, ring)),
            out_shape=shapes,
            in_specs=[any_spec] * 7,
            out_specs=(vmem_spec,) * 3,
            scratch_shapes=[
                pltpu.VMEM((2, rows, head), low), pltpu.VMEM((HOPS, 2, rows, head), low),
                pltpu.VMEM((2, flat, head), low), pltpu.VMEM((HOPS, 2, flat, head), low), pltpu.VMEM((2, flat, head), low),
                pltpu.VMEM((flat, head), low),
                pltpu.VMEM((2, flat), full), pltpu.VMEM((HOPS, 2, flat), full),
                pltpu.VMEM((heads, rows), full), pltpu.VMEM((1, cu_seqlens.shape[0]), jnp.int32),
                pltpu.VMEM((HOPS + 1, 1, flat), full),
                pltpu.VMEM((head, rows), low), pltpu.VMEM((head, flat), full),
                pltpu.VMEM((rows, head), full), pltpu.VMEM((rows, head), full),
                dma((7,)),
                dma((HOPS, CHUNKS)), dma((HOPS, CHUNKS)), dma((HOPS, CHUNKS)), dma((HOPS, CHUNKS)),
                dma((CHUNKS,)), dma((CHUNKS,)), dma((CHUNKS,)), dma((HOPS,)), dma((HOPS,)),
            ],
            compiler_params=pltpu.CompilerParams(collective_id=0, has_side_effects=True),
        )(queries.reshape(flat, head), keys, values, attn_out.reshape(flat, head), d_out.reshape(flat, head),
          logsumexp.T, cu_seqlens.reshape(1, -1))
        d_query, d_key, d_value = pl.pallas_call(
            store_kernel, out_shape=shapes, in_specs=[vmem_spec] * 3, out_specs=(any_spec,) * 3, scratch_shapes=[dma((3,))],
        )(*grads)
        return d_query.reshape(rows, heads, head), d_key, d_value

    seq_spec = P(("dp", "cpo", "cp"))
    return jax.shard_map(local, mesh=mesh, in_specs=(seq_spec,) * 6 + (P("dp"),), out_specs=(seq_spec,) * 3, check_vma=False)
```

time: 56.5 us -> 39.7 us (0.70)
  the two profiles are of different devices: /device:TPU:1 before, /device:TPU:94 now
where the time goes in v2:
time: 39.7 us; the launch traced here: 39.6 us
  Pallas kernels  38.9 us (98%)
  between operations  0.64 us (2%)
    pallas_call x1, Pallas kernels, local(): pl.pallas_call(functools.partial(backward_kernel, (outer, inner, rows, he...  37.1 us
    pallas_call x1, Pallas kernels, local(): pl.pallas_call(store_kernel, out_shape=shapes, in_specs=[vmem_spec] * 3,...  1.86 us

profile of v2, /device:TPU:94, one launch (start us, length us, event | category | flops | bytes accessed | tf_op | source)
XLA Modules:
  0.0 39.6 jit_solution(13043123199488514850)
XLA Ops:
  0.6 37.1 %shard_map.94 = (bf16[1024,128]{1,0:T(8,128)(2,1)}, bf16[512,128]{1,0:T(8,128)(2,1)}, bf16[512,128]{1,0:T(8,128)(2,1)}) custom-call(bf16[1024,128]{1,0:T(8,128)(2,1)} %bitcast.6, bf16[512,128]{1,0:T(8,128)(2,1)} %k_hbm.1, bf16[512,128]{1,0:T(8,128)(2,1)} %v_hbm.1, bf16[1024,128]{1,0:T(8,128)(2,1)} %bitcast.7, bf16[1024,128]{1,0:T(8,128)(2,1)} %bitcast.8, ...), custom_call_target="tpu_custom_call" | custom-call | tf_op jit(solution)/shard_map/pallas_call | solution.py:347
  37.7 1.9 %shard_map.95 = (bf16[1024,128]{1,0:T(8,128)(2,1)}, bf16[512,128]{1,0:T(8,128)(2,1)}, bf16[512,128]{1,0:T(8,128)(2,1)}) custom-call(bf16[1024,128]{1,0:T(8,128)(2,1)} %get-tuple-element.9.dq_in, bf16[512,128]{1,0:T(8,128)(2,1)} %get-tuple-element.10.dk_in, bf16[512,128]{1,0:T(8,128)(2,1)} %get-tuple-element.11.dv_in), custom_call_target="tpu_custom_call" | custom-call | tf_op jit(solution)/shard_map/pallas_call | solution.py:368

commit v3 on v2

--- a/solution.py
+++ b/solution.py
@@ -11,7 +11,8 @@
 MESH = pl.DeviceIdType.MESH
 HOPS = 3
 CHUNKS = 4
-FAR = (1, 2, 3)
+FAR = (0, 1, 2)
+ORDER = (3, 0, 1, 2)
 VIA = 2
 LOG2E = math.log2(math.e)
 NT = (((1,), (1,)), ((), ()))
@@ -52,9 +53,11 @@
 
     barrier = pltpu.get_barrier_semaphore()
     arrivals = 0
-    for step in (-4, -3, -1, 1, 3, 4):
+    for step in (-4, -3, -2, -1, 1, 2, 3, 4):
         peer = rank + step
         known = (peer >= 0) & (peer < group)
+        if abs(step) > HOPS:
+            known = known & (column == VIA)
 
         @pl.when(known)
         def _():
@@ -80,11 +83,10 @@
             device_id=device(rank - 1), device_id_type=MESH)
 
     def ld_copy(hop):
-        source = ld_own if hop == 0 else ld_in.at[hop - 1]
-        return pltpu.make_async_remote_copy(
-            src_ref=source, dst_ref=ld_in.at[hop],
+        return pltpu.make_async_remote_copy(
+            src_ref=ld_own, dst_ref=ld_in.at[hop],
             send_sem=ld_send.at[hop], recv_sem=ld_recv.at[hop],
-            device_id=device(rank - 1), device_id_type=MESH)
+            device_id=device(rank - hop - 1), device_id_type=MESH)
 
     def far_copy(chunk):
         part = pl.ds(chunk * lanes, lanes)
@@ -111,6 +113,7 @@
     gets_kv = [rank >= hop + 1 for hop in range(HOPS)]
     sends_qd = [(rank >= 1) & (rank + hop < group) for hop in range(HOPS)]
     gets_qd = [rank + hop + 1 < group for hop in range(HOPS)]
+    sends_ld = [rank >= hop + 1 for hop in range(HOPS)]
     is_via = column == VIA
     sends_far = (rank >= HOPS) & ~is_via
     sends_via = (rank >= HOPS + 1) & is_via
@@ -129,7 +132,11 @@
 
     @pl.when(sends_qd[0])
     def _():
-        qd_copy(0, 0).start()
+        qd_copy(0, ORDER[0]).start()
+
+    @pl.when(sends_far)
+    def _():
+        far_copy(FAR[0]).start()
 
     @pl.when(sends_via)
     def _():
@@ -177,10 +184,14 @@
 
     lax.fori_loop(0, (HOPS + 1) * flat // head, fill_starts, 0)
 
+    for hop in range(HOPS):
+        @pl.when(sends_ld[hop])
+        def _():
+            ld_copy(hop).start()
+
     @pl.when(sends_qd[0])
     def _():
-        ld_copy(0).start()
-        for chunk in range(1, CHUNKS):
+        for chunk in ORDER[1:]:
             qd_copy(0, chunk).start()
 
     dk_acc[...] = jnp.zeros_like(dk_acc)
@@ -251,10 +262,16 @@
         def _():
             ld_copy(hop).wait_recv()
 
-        if hop + 1 < HOPS:
-            @pl.when(sends_qd[hop + 1])
-            def _():
-                ld_copy(hop + 1).start()
+    def far_goes(index):
+        @pl.when(sends_far)
+        def _():
+            far_copy(FAR[index]).start()
+
+    def via_passes(index):
+        @pl.when(passes)
+        def _():
+            via_copy(FAR[index]).wait_recv()
+            pass_copy(FAR[index]).start()
 
     def queries_used(hop, chunk):
         @pl.when(gets_qd[hop])
@@ -262,41 +279,48 @@
             k_from = chunk * span if hop + 1 == HOPS else 0
             tile(kv_own, k_from, rows, qd_in.at[hop], ld_in.at[hop], chunk, 0, hop + 1, False, True)
 
-    for slot in range(2 * CHUNKS):
-        if slot < HOPS * CHUNKS // 2:
-            keys_arrive(slot // 2, (2 * (slot % 2), 2 * (slot % 2) + 1))
-        hop, chunk = slot // CHUNKS, slot % CHUNKS
-        queries_arrive(hop, chunk)
-        if chunk == 0:
+    def queries(hop, index):
+        queries_arrive(hop, ORDER[index])
+        if index == 0:
             stats_arrive(hop)
-        if slot == CHUNKS - 1:
-            @pl.when(sends_far)
-            def _():
-                for far in FAR:
-                    far_copy(far).start()
-
-            @pl.when(passes)
-            def _():
-                for far in FAR:
-                    via_copy(far).wait_recv()
-                    pass_copy(far).start()
-        queries_used(hop, chunk)
-        if slot % 2 == 1 and slot // 2 < HOPS:
-            keys_used(slot // 2)
-        if slot == 2 * HOPS - 1:
-            for part in range(flat // head):
-                piece = slice(part * head, (part + 1) * head)
-                dq_out[piece, :] = (scale * dq_t[:, piece].T).astype(jnp.bfloat16)
-        if slot == 2 * HOPS - 1:
+        queries_used(hop, ORDER[index])
+
+    def far_queries(index):
+        queries_arrive(HOPS - 1, FAR[index])
+        if index == 0:
             stats_arrive(HOPS - 1)
-        if slot >= 2 * HOPS:
-            far = FAR[slot - 2 * HOPS]
-            queries_arrive(HOPS - 1, far)
-            queries_used(HOPS - 1, far)
-    rest = [chunk for chunk in range(CHUNKS) if chunk not in FAR]
-    for chunk in rest + list(FAR[2 * CHUNKS - 2 * HOPS:]):
-        queries_arrive(HOPS - 1, chunk)
-        queries_used(HOPS - 1, chunk)
+        queries_used(HOPS - 1, FAR[index])
+
+    keys_arrive(0, (0, 1))
+    queries(0, 0)
+    keys_arrive(0, (2, 3))
+    far_goes(1)
+    via_passes(0)
+    queries(0, 1)
+    keys_used(0)
+    queries(0, 2)
+    far_queries(0)
+    keys_arrive(1, (0, 1))
+    via_passes(1)
+    queries(0, 3)
+    keys_arrive(1, (2, 3))
+    far_goes(2)
+    via_passes(2)
+    queries(1, 0)
+    keys_used(1)
+    queries(1, 1)
+    far_queries(1)
+    keys_arrive(2, (0, 1))
+    queries(1, 2)
+    keys_arrive(2, (2, 3))
+    queries(1, 3)
+    keys_used(2)
+    for part in range(flat // head):
+        piece = slice(part * head, (part + 1) * head)
+        dq_out[piece, :] = (scale * dq_t[:, piece].T).astype(jnp.bfloat16)
+    far_queries(2)
+    queries_arrive(HOPS - 1, ORDER[0])
+    queries_used(HOPS - 1, ORDER[0])
 
     dk_out[...] = (scale * dk_acc[...]).astype(jnp.bfloat16)
     dv_out[...] = dv_acc[...].astype(jnp.bfloat16)
@@ -308,8 +332,11 @@
 
         @pl.when(sends_qd[hop])
         def _():
-            for chunk in range(CHUNKS) if hop + 1 < HOPS else rest:
+            for chunk in ORDER if hop + 1 < HOPS else ORDER[:1]:
                 qd_copy(hop, chunk).wait_send()
+
+        @pl.when(sends_ld[hop])
+        def _():
             ld_copy(hop).wait_send()
 
     @pl.when(sends_far | sends_via)
@@ -346,7 +373,7 @@
         shapes = (jax.ShapeDtypeStruct((flat, head), low), jax.ShapeDtypeStruct((rows, head), low), jax.ShapeDtypeStruct((rows, head), low))
         grads = pl.pallas_call(
             functools.partial(backward_kernel, (outer, inner, rows, heads, head, ring)),
-            out_shape=shapes,
+            out_shape=tuple(pltpu.VMEM(shape.shape, low) for shape in shapes),
             in_specs=[any_spec] * 7,
             out_specs=(vmem_spec,) * 3,
             scratch_shapes=[
@@ -367,7 +394,7 @@
           logsumexp.T, cu_seqlens.reshape(1, -1))
         d_query, d_key, d_value = pl.pallas_call(
             store_kernel, out_shape=shapes, in_specs=[vmem_spec] * 3, out_specs=(any_spec,) * 3, scratch_shapes=[dma((3,))],
-        )(*grads)
+        )(*(pltpu.with_memory_space_constraint(grad, pltpu.VMEM) for grad in grads))
         return d_query.reshape(rows, heads, head), d_key, d_value
 
     seq_spec = P(("dp", "cpo", "cp"))

time: 39.7 us -> 36.5 us (0.919)
  Pallas kernels: 38.9 us -> 35.7 us
    pallas_call x1, Pallas kernels: 37.1 us -> 34.9 us  [local(): pl.pallas_call(functools.partial(backward_kernel, (outer, inner, rows, he...]
    pallas_call x1, Pallas kernels: 1.86 us -> 0.81 us  [local(): pl.pallas_call(store_kernel, out_shape=shapes, in_specs=[vmem_spec] * 3,...]
where the time goes in v3:
time: 36.5 us; the launch traced here: 36.4 us
  Pallas kernels  35.7 us (98%)
  between operations  0.64 us (2%)
    pallas_call x1, Pallas kernels, local(): pl.pallas_call(functools.partial(backward_kernel, (outer, inner, rows, he...  34.9 us
    pallas_call x1, Pallas kernels, local(): pl.pallas_call(store_kernel, out_shape=shapes, in_specs=[vmem_spec] * 3,...  0.81 us

profile of v3, /device:TPU:94, one launch (start us, length us, event | category | flops | bytes accessed | tf_op | source)
XLA Modules:
  0.0 36.4 jit_solution(9744960197875826513)
XLA Ops:
  0.6 34.9 %shard_map.94 = (bf16[1024,128]{1,0:T(8,128)(2,1)S(1)}, bf16[512,128]{1,0:T(8,128)(2,1)S(1)}, bf16[512,128]{1,0:T(8,128)(2,1)S(1)}) custom-call(bf16[1024,128]{1,0:T(8,128)(2,1)} %bitcast.6, bf16[512,128]{1,0:T(8,128)(2,1)} %k_hbm.1, bf16[512,128]{1,0:T(8,128)(2,1)} %v_hbm.1, bf16[1024,128]{1,0:T(8,128)(2,1)} %bitcast.7, bf16[1024,128]{1,0:T(8,128)(2,1)} %bitcast.8, ...), custom_call_target="tpu_custom_call" | custom-call | tf_op jit(solution)/shard_map/pallas_call | solution.py:374
  35.6 0.8 %shard_map.95 = (bf16[1024,128]{1,0:T(8,128)(2,1)}, bf16[512,128]{1,0:T(8,128)(2,1)}, bf16[512,128]{1,0:T(8,128)(2,1)}) custom-call(bf16[1024,128]{1,0:T(8,128)(2,1)S(1)} %get-tuple-element.9.dq_in, bf16[512,128]{1,0:T(8,128)(2,1)S(1)} %get-tuple-element.10.dk_in, bf16[512,128]{1,0:T(8,128)(2,1)S(1)} %get-tuple-element.11.dv_in), custom_call_target="tpu_custom_call" | custom-call | tf_op jit(solution)/shard_map/pallas_call | solution.py:395

commit v4 on v0

v4 whole, which is shorter than its diff:
```python
import functools
import math

import jax
import jax.numpy as jnp
from jax import lax
from jax.experimental import pallas as pl
from jax.experimental.pallas import tpu as pltpu
from jax.sharding import PartitionSpec as P

MESH = pl.DeviceIdType.MESH
SHARDS = 5
KV_CHUNKS = 2
QD_CHUNKS = 4
LOG2E = math.log2(math.e)
NT = (((1,), (1,)), ((), ()))
NN = (((1,), (0,)), ((), ()))


def dot(lhs, rhs, dims):
    return lax.dot_general(lhs, rhs, dims, preferred_element_type=jnp.float32)


def backward_kernel(sizes, q_hbm, k_hbm, v_hbm, o_hbm, do_hbm, lse_hbm, cu_hbm, dq_out, dkv_out,
                    kv_s, kv_w, qd_s, qd_w, ld_s, ld_w, o_buf, lse_buf, cu_buf, starts, key_t, dq_t, dk_acc, dv_acc, dq_fin, dkv_fin,
                    load_sem, guest_send, guest_recv, fwd_send, fwd_recv, right_send, right_recv, left_send, left_recv, back_send, back_recv):
    outer, inner, rows, heads, head = sizes
    group = outer * inner
    pairs = group // 2
    scale = head ** -0.5
    flat = rows * heads
    k_part = rows // KV_CHUNKS
    lanes = flat // QD_CHUNKS
    span = rows // QD_CHUNKS
    bounds = cu_buf.shape[1]
    rank = lax.axis_index("cpo") * inner + lax.axis_index("cp")

    def resident(pair):
        return (pair + pair // (inner // 2) + 1) % 2

    def host(pair):
        return 2 * pair + resident(pair)

    def helper(pair):
        return (host(pair) + inner) % group

    is_host = rank % 2 == resident(rank // 2)
    is_helper = rank % 2 != resident(rank // 2)
    pair = jnp.where(is_host, rank // 2, ((rank + inner) % group) // 2)
    res = resident(pair)
    gst = 1 - res
    guest = 2 * pair + gst
    own = jnp.where(is_host, res, 2)
    prev_res, next_res = resident(pair - 1), resident(pair + 1)
    has_prev, has_prev2 = pair >= 1, pair >= 2
    has_next, has_next2 = pair + 1 < pairs, pair + 2 < pairs
    my_host = 2 * (rank // 2) + resident(rank // 2)

    def device(index):
        return (0, index // inner, index % inner)

    def remote(source, target, send, recv, index):
        return pltpu.make_async_remote_copy(src_ref=source, dst_ref=target, send_sem=send, recv_sem=recv,
                                            device_id=device(index), device_id_type=MESH)

    loads = [
        pltpu.make_async_copy(k_hbm, kv_s.at[own, 0], load_sem.at[0]),
        pltpu.make_async_copy(v_hbm, kv_s.at[own, 1], load_sem.at[1]),
        pltpu.make_async_copy(q_hbm, qd_s.at[own, 0], load_sem.at[2]),
        pltpu.make_async_copy(do_hbm, qd_s.at[own, 1], load_sem.at[3]),
        pltpu.make_async_copy(o_hbm, o_buf, load_sem.at[4]),
        pltpu.make_async_copy(lse_hbm, lse_buf, load_sem.at[5]),
        pltpu.make_async_copy(cu_hbm, cu_buf, load_sem.at[6]),
    ]
    for load in loads:
        load.start()

    barrier = pltpu.get_barrier_semaphore()
    everyone = rank >= 0
    peers = [
        (is_host, helper(pair)), (is_host, guest), (is_helper, host(pair)), (is_helper, guest),
        (is_helper, my_host), (is_helper, (my_host + inner) % group),
        (everyone & has_next, host(pair + 1)), (everyone & has_next2, host(pair + 2)),
        (is_host & has_prev, host(pair - 1)), (is_host & has_prev2, host(pair - 2)),
        (is_host & has_prev, helper(pair - 1)), (is_host & has_prev2, helper(pair - 2)),
    ]
    arrivals = 0
    for known, peer in peers:
        @pl.when(known)
        def _():
            pl.semaphore_signal(barrier, inc=1, device_id=device(peer), device_id_type=MESH)

        arrivals = arrivals + jnp.where(known, 1, 0)
    pl.semaphore_wait(barrier, arrivals)

    def kv_rows(chunk):
        return pl.ds(chunk * k_part, k_part)

    def qd_rows(chunk):
        if isinstance(chunk, int):
            return pl.ds(chunk * lanes, lanes)
        return pl.ds(pl.multiple_of(chunk * lanes, lanes), lanes)

    LD = KV_CHUNKS + QD_CHUNKS

    place = jnp.where(is_host, gst, rank % 2)

    def guest_kv(chunk):
        part = kv_rows(chunk)
        return remote(kv_s.at[2, :, part], kv_s.at[place, :, part], guest_send.at[chunk], guest_recv.at[chunk], my_host)

    def guest_qd(chunk):
        part = qd_rows(chunk)
        return remote(qd_s.at[2, :, part], qd_s.at[place, :, part], guest_send.at[KV_CHUNKS + chunk], guest_recv.at[KV_CHUNKS + chunk], my_host)

    def guest_ld():
        return remote(ld_s.at[2], ld_s.at[place], guest_send.at[LD], guest_recv.at[LD], my_host)

    def fwd_kv(slot, chunk):
        part = kv_rows(chunk)
        return remote(kv_s.at[slot, :, part], kv_s.at[slot, :, part], fwd_send.at[slot, chunk], fwd_recv.at[slot, chunk], helper(pair))

    def fwd_qd(slot, chunk):
        part = qd_rows(chunk)
        return remote(qd_s.at[slot, :, part], qd_s.at[slot, :, part], fwd_send.at[slot, KV_CHUNKS + chunk], fwd_recv.at[slot, KV_CHUNKS + chunk], helper(pair))

    def fwd_ld(slot):
        return remote(ld_s.at[slot], ld_s.at[slot], fwd_send.at[slot, LD], fwd_recv.at[slot, LD], helper(pair))

    def right1(slot, chunk):
        part = kv_rows(chunk)
        return remote(kv_s.at[slot, :, part], kv_w.at[slot, :, part], right_send.at[slot, chunk], right_recv.at[slot, chunk], host(pair + 1))

    def right2(chunk):
        part = kv_rows(chunk)
        return remote(kv_s.at[1, :, part], kv_w.at[2, :, part], right_send.at[2, chunk], right_recv.at[2, chunk], host(pair + 2))

    def left1(slot, chunk):
        part = qd_rows(chunk)
        return remote(qd_s.at[slot, :, part], qd_w.at[slot, :, part], left_send.at[slot, chunk], left_recv.at[slot, chunk], helper(pair - 1))

    def left2(chunk):
        part = qd_rows(chunk)
        return remote(qd_s.at[0, :, part], qd_w.at[2, :, part], left_send.at[2, chunk], left_recv.at[2, chunk], helper(pair - 2))

    def left1_ld(slot):
        return remote(ld_s.at[slot], ld_w.at[slot], left_send.at[slot, QD_CHUNKS], left_recv.at[slot, QD_CHUNKS], helper(pair - 1))

    def left2_ld():
        return remote(ld_s.at[0], ld_w.at[2], left_send.at[2, QD_CHUNKS], left_recv.at[2, QD_CHUNKS], helper(pair - 2))

    def back_dq():
        return remote(dq_fin.at[gst], dq_out, back_send.at[0], back_recv.at[0], guest)

    def back_dkv(slot, index, target):
        return remote(dkv_fin.at[slot], dkv_out, back_send.at[index], back_recv.at[1], target)

    def when(cond, *starts_of):
        @pl.when(cond)
        def _():
            for item in starts_of:
                item().start()

    loads[0].wait()
    loads[1].wait()
    for chunk in range(KV_CHUNKS):
        when(is_helper, lambda: guest_kv(chunk))
        when(is_host & has_next, lambda: right1(res, chunk))
        when(is_host, lambda: fwd_kv(res, chunk))
        when(is_host & has_next2 & (res == 1), lambda: right2(chunk))
    loads[2].wait()
    loads[3].wait()
    for chunk in range(QD_CHUNKS):
        when(is_host, lambda: fwd_qd(res, chunk))
    for chunk in range(QD_CHUNKS // 2):
        when(is_host & has_prev2 & (res == 0), lambda: left2(chunk))
    loads[4].wait()
    loads[5].wait()
    loads[6].wait()

    row_id = lax.broadcasted_iota(jnp.int32, (head, heads * head), 0)
    lane_id = lax.broadcasted_iota(jnp.int32, (head, heads * head), 1)
    for part in range(rows // head):
        piece = slice(part * head, (part + 1) * head)
        wide = jnp.zeros((head, heads * head), jnp.float32)
        for g in range(heads):
            column_g = jnp.broadcast_to(lse_buf[g:g + 1, piece], (head, head)).T
            wide = jnp.where(lane_id == row_id * heads + g, jnp.concatenate([column_g] * heads, axis=1), wide)
        ld_s[own, 0:1, part * heads * head:(part + 1) * heads * head] = jnp.sum(wide, axis=0, keepdims=True) * LOG2E
    for part in range(flat // head):
        piece = slice(part * head, (part + 1) * head)
        prod = qd_s[own, 1, piece, :].astype(jnp.float32) * o_buf[piece, :].astype(jnp.float32)
        ld_s[own, 1:2, piece] = jnp.sum(prod.T, axis=0, keepdims=True)

    first = (pair * (2 * rows)).astype(jnp.float32)
    cuts = cu_buf[...].astype(jnp.float32)
    cut_cols = []
    for base in range(0, bounds, head):
        width = min(head, bounds - base)
        row = cuts[:, base:base + width]
        if width < head:
            row = jnp.concatenate([row, jnp.zeros((1, head - width), jnp.float32)], axis=1)
        cut_cols.append(jnp.broadcast_to(row, (head, head)).T - first)
    lane = lax.broadcasted_iota(jnp.int32, (1, head), 1)

    def fill_starts(step, _):
        lane_base = pl.multiple_of((step % (flat // head)) * head, head)
        shard = step // (flat // head)
        token = ((lane + lane_base) // heads + shard * rows).astype(jnp.float32)
        best = jnp.full((head, head), -1e9, jnp.float32)
        for col in cut_cols:
            best = jnp.maximum(best, jnp.where(col <= token, col, -1e9))
        starts[shard, :, pl.ds(lane_base, head)] = jnp.max(best, axis=0, keepdims=True)
        return 0

    lax.fori_loop(0, 2 * (flat // head), fill_starts, 0)

    when(is_helper, guest_ld)
    when(is_host, lambda: fwd_ld(res))
    when(is_host & has_prev, lambda: left1_ld(res))
    when(is_host & has_prev2 & (res == 0), left2_ld)
    for chunk in range(QD_CHUNKS):
        when(is_helper, lambda: guest_qd(chunk))
        when(is_host & has_prev, lambda: left1(res, chunk))

    def scores(kv, key_rows, key_off, qd, ld, part, start, token_off):
        keys, vals = kv[0, key_rows, :], kv[1, key_rows, :]
        qry, dout = qd[0, part, :], qd[1, part, :]
        score = dot(keys, qry, NT)
        grad = dot(vals, dout, NT)
        lse, row_dot = ld[0:1, part], ld[1:2, part]
        key_pos = lax.broadcasted_iota(jnp.int32, score.shape, 0).astype(jnp.float32)
        keep = key_pos >= start[:, part] - key_off
        if token_off is not None:
            token = lax.broadcasted_iota(jnp.int32, (1, lanes), 1) // heads + token_off
            keep = keep & (key_pos <= token.astype(jnp.float32))
        prob = jnp.where(keep, jnp.exp2(score * (scale * LOG2E) - lse), 0.0)
        dsc = (prob * (grad - row_dot)).astype(jnp.bfloat16)
        return prob, dsc, qry, dout

    def q_tile(kv, k_from, k_to, key_off, q_slot, chunk, token_off=None):
        part, key_rows = qd_rows(chunk), pl.ds(k_from, k_to - k_from)
        _, dsc, _, _ = scores(kv, key_rows, key_off + k_from, qd_s.at[q_slot], ld_s.at[q_slot], part, starts.at[q_slot], token_off)
        dq_t[q_slot, :, part] += dot(key_t[:, k_from:k_to], dsc, NN)

    def k_tile(k_slot, k_from, k_to, qd, ld, q_shard, chunk, token_off=None):
        part, key_rows = qd_rows(chunk), pl.ds(k_from, k_to - k_from)
        key_off = (k_slot * rows + k_from) * 1.0
        prob, dsc, qry, dout = scores(kv_s.at[k_slot], key_rows, key_off, qd, ld, part, starts.at[q_shard], token_off)
        dv_acc[k_slot, key_rows, :] += dot(prob.astype(jnp.bfloat16), dout, NN)
        dk_acc[k_slot, key_rows, :] += dot(dsc, qry, NN)

    def finish_dq(slot, target):
        for part in range(flat // head):
            piece = slice(part * head, (part + 1) * head)
            target[piece, :] = (scale * dq_t[slot, :, piece].T).astype(jnp.bfloat16)

    def finish_dkv(slot):
        dkv_fin[slot, 0, :, :] = (scale * dk_acc[slot, :, :]).astype(jnp.bfloat16)
        dkv_fin[slot, 1, :, :] = dv_acc[slot, :, :].astype(jnp.bfloat16)

    @pl.when(is_host)
    def _():
        dq_t[...] = jnp.zeros_like(dq_t)

        def diagonal(slot):
            key_t[...] = kv_s[slot, 0, :, :].T
            for chunk in range(QD_CHUNKS):
                q_tile(kv_s.at[slot], 0, (chunk + 1) * span, slot * rows * 1.0, slot, chunk, chunk * span)

        diagonal(res)
        for chunk in range(KV_CHUNKS):
            guest_kv(chunk).wait_recv()
            when(has_next, lambda: right1(gst, chunk))
            fwd_kv(gst, chunk).start()
            when(has_next2 & (gst == 1), lambda: right2(chunk))
        guest_ld().wait_recv()
        fwd_ld(gst).start()
        when(has_prev, lambda: left1_ld(gst))
        when(has_prev2 & (gst == 0), left2_ld)
        for chunk in range(QD_CHUNKS // 2, QD_CHUNKS):
            when(has_prev2 & (res == 0), lambda: left2(chunk))

        @pl.when(has_prev)
        def _():
            for chunk in range(KV_CHUNKS):
                right1(prev_res, chunk).wait_recv()
            key_t[...] = kv_w[prev_res, 0, :, :].T

        prev_off = (prev_res - 2) * rows * 1.0
        late_off = (-1 - prev_res) * rows * 1.0

        def pass_queries(chunk, _):
            guest_qd(chunk).wait_recv()
            when(has_prev, lambda: left1(gst, chunk))
            fwd_qd(gst, chunk).start()
            when(has_prev2 & (gst == 0), lambda: left2(chunk))

            @pl.when(has_prev)
            def _():
                q_tile(kv_w.at[prev_res], 0, rows, prev_off, res, chunk)
                q_tile(kv_w.at[prev_res], 0, rows, prev_off, gst, chunk)

            return 0

        lax.fori_loop(0, QD_CHUNKS, pass_queries, 0)
        diagonal(gst)
        key_t[...] = kv_s[0, 0, :, :].T
        for chunk in range(QD_CHUNKS):
            q_tile(kv_s.at[0], 0, rows, 0.0, 1, chunk)

        @pl.when(has_prev2)
        def _():
            for chunk in range(KV_CHUNKS):
                right2(chunk).wait_recv()
            key_t[...] = kv_w[2, 0, :, :].T
            for chunk in range(QD_CHUNKS):
                q_tile(kv_w.at[2], chunk * span, rows, -3.0 * rows, 0, chunk)

        def late_keys(slot):
            @pl.when(has_prev)
            def _():
                def two(step, _):
                    q_tile(kv_w.at[1 - prev_res], 0, rows, late_off, slot, 2 * step)
                    q_tile(kv_w.at[1 - prev_res], 0, rows, late_off, slot, 2 * step + 1)
                    return 0

                lax.fori_loop(0, QD_CHUNKS // 2, two, 0)

        @pl.when(has_prev)
        def _():
            for chunk in range(KV_CHUNKS):
                right1(1 - prev_res, chunk).wait_recv()
            key_t[...] = kv_w[1 - prev_res, 0, :, :].T

        late_keys(gst)
        finish_dq(gst, dq_fin.at[gst])
        late_keys(res)
        back_dq().start()
        finish_dq(res, dq_out)

        for chunk in range(KV_CHUNKS):
            fwd_kv(res, chunk).wait_send()
            fwd_kv(gst, chunk).wait_send()
        for chunk in range(QD_CHUNKS):
            fwd_qd(res, chunk).wait_send()
            fwd_qd(gst, chunk).wait_send()
        fwd_ld(res).wait_send()
        fwd_ld(gst).wait_send()

        @pl.when(has_next)
        def _():
            for chunk in range(KV_CHUNKS):
                right1(0, chunk).wait_send()
                right1(1, chunk).wait_send()

        @pl.when(has_next2)
        def _():
            for chunk in range(KV_CHUNKS):
                right2(chunk).wait_send()

        @pl.when(has_prev)
        def _():
            for slot in range(2):
                for chunk in range(QD_CHUNKS):
                    left1(slot, chunk).wait_send()
                left1_ld(slot).wait_send()

        @pl.when(has_prev2)
        def _():
            for chunk in range(QD_CHUNKS):
                left2(chunk).wait_send()
            left2_ld().wait_send()

        back_dq().wait_send()
        back_dkv(0, 1, guest).wait_recv()

    @pl.when(is_helper)
    def _():
        lax.fori_loop(2 * (flat // head), SHARDS * (flat // head), fill_starts, 0)
        dk_acc[...] = jnp.zeros_like(dk_acc)
        dv_acc[...] = jnp.zeros_like(dv_acc)

        def diagonal(slot):
            for chunk in range(QD_CHUNKS):
                k_tile(slot, 0, (chunk + 1) * span, qd_s.at[slot], ld_s.at[slot], slot, chunk, chunk * span)

        for chunk in range(KV_CHUNKS):
            fwd_kv(res, chunk).wait_recv()
        for chunk in range(QD_CHUNKS):
            fwd_qd(res, chunk).wait_recv()
        fwd_ld(res).wait_recv()
        diagonal(res)
        for chunk in range(KV_CHUNKS):
            fwd_kv(gst, chunk).wait_recv()

        def queries(slot):
            @pl.when(has_next)
            def _():
                left1_ld(slot).wait_recv()

                def one(chunk, _):
                    left1(slot, chunk).wait_recv()
                    k_tile(gst, 0, rows, qd_w.at[slot], ld_w.at[slot], slot + 2, chunk)
                    k_tile(res, 0, rows, qd_w.at[slot], ld_w.at[slot], slot + 2, chunk)
                    return 0

                lax.fori_loop(0, QD_CHUNKS, one, 0)

        queries(next_res)
        for chunk in range(QD_CHUNKS):
            fwd_qd(gst, chunk).wait_recv()
        fwd_ld(gst).wait_recv()
        diagonal(gst)
        for chunk in range(QD_CHUNKS):
            k_tile(0, 0, rows, qd_s.at[1], ld_s.at[1], 1, chunk)

        @pl.when(has_next2)
        def _():
            left2_ld().wait_recv()
            for chunk in range(QD_CHUNKS):
                left2(chunk).wait_recv()
                k_tile(1, chunk * span, rows, qd_w.at[2], ld_w.at[2], 4, chunk)

        queries(1 - next_res)
        finish_dkv(gst)
        finish_dkv(res)
        back_dkv(gst, 1, guest).start()
        back_dkv(res, 2, host(pair)).start()

        for chunk in range(KV_CHUNKS):
            guest_kv(chunk).wait_send()
        for chunk in range(QD_CHUNKS):
            guest_qd(chunk).wait_send()
        guest_ld().wait_send()
        back_dkv(gst, 1, guest).wait_send()
        back_dkv(res, 2, host(pair)).wait_send()
        back_dq().wait_recv()
        back_dkv(0, 1, guest).wait_recv()


def store_kernel(dq_in, dkv_in, dq_hbm, dk_hbm, dv_hbm, sem):
    copies = [pltpu.make_async_copy(source, target, sem.at[index])
              for index, (source, target) in enumerate(((dq_in, dq_hbm), (dkv_in.at[0], dk_hbm), (dkv_in.at[1], dv_hbm)))]
    for copy in copies:
        copy.start()
    for copy in copies:
        copy.wait()


def solution(mesh):
    outer, inner = mesh.shape["cpo"], mesh.shape["cp"]

    def local(queries, keys, values, attn_out, logsumexp, d_out, cu_seqlens):
        rows, heads, head = queries.shape
        flat = rows * heads
        low, full = jnp.bfloat16, jnp.float32
        any_spec = pl.BlockSpec(memory_space=pl.ANY)
        vmem_spec = pl.BlockSpec(memory_space=pltpu.VMEM)
        dma = pltpu.SemaphoreType.DMA
        moves = KV_CHUNKS + QD_CHUNKS + 1
        grads = pl.pallas_call(
            functools.partial(backward_kernel, (outer, inner, rows, heads, head)),
            out_shape=(pltpu.VMEM((flat, head), low), pltpu.VMEM((2, rows, head), low)),
            in_specs=[any_spec] * 7,
            out_specs=(vmem_spec,) * 2,
            scratch_shapes=[
                pltpu.VMEM((3, 2, rows, head), low), pltpu.VMEM((3, 2, rows, head), low),
                pltpu.VMEM((3, 2, flat, head), low), pltpu.VMEM((3, 2, flat, head), low),
                pltpu.VMEM((3, 2, flat), full), pltpu.VMEM((3, 2, flat), full),
                pltpu.VMEM((flat, head), low), pltpu.VMEM((heads, rows), full), pltpu.VMEM((1, cu_seqlens.shape[0]), jnp.int32),
                pltpu.VMEM((SHARDS, 1, flat), full), pltpu.VMEM((head, rows), low),
                pltpu.VMEM((2, head, flat), full), pltpu.VMEM((2, rows, head), full), pltpu.VMEM((2, rows, head), full),
                pltpu.VMEM((2, flat, head), low), pltpu.VMEM((2, 2, rows, head), low),
                dma((7,)), dma((moves,)), dma((moves,)), dma((2, moves)), dma((2, moves)),
                dma((3, KV_CHUNKS)), dma((3, KV_CHUNKS)), dma((3, QD_CHUNKS + 1)), dma((3, QD_CHUNKS + 1)), dma((3,)), dma((2,)),
            ],
            compiler_params=pltpu.CompilerParams(collective_id=0, has_side_effects=True),
        )(queries.reshape(flat, head), keys, values, attn_out.reshape(flat, head), d_out.reshape(flat, head),
          logsumexp.T, cu_seqlens.reshape(1, -1))
        d_query, d_key, d_value = pl.pallas_call(
            store_kernel,
            out_shape=(jax.ShapeDtypeStruct((flat, head), low), jax.ShapeDtypeStruct((rows, head), low), jax.ShapeDtypeStruct((rows, head), low)),
            in_specs=[vmem_spec] * 2, out_specs=(any_spec,) * 3, scratch_shapes=[dma((3,))],
        )(*(pltpu.with_memory_space_constraint(grad, pltpu.VMEM) for grad in grads))
        return d_query.reshape(rows, heads, head), d_key, d_value

    seq_spec = P(("dp", "cpo", "cp"))
    return jax.shard_map(local, mesh=mesh, in_specs=(seq_spec,) * 6 + (P("dp"),), out_specs=(seq_spec,) * 3, check_vma=False)
```

time: 236 us -> 43.5 us (0.18)
  the two profiles are of different devices: /device:TPU:94 before, /device:TPU:126 now
where the time goes in v4:
time: 43.5 us; the launch traced here: 43.4 us
  Pallas kernels  42.8 us (98%)
  between operations  0.64 us (1%)
    pallas_call x1, Pallas kernels, local(): pl.pallas_call(functools.partial(backward_kernel, (outer, inner, rows, he...  41.9 us

profile of v4, /device:TPU:126, one launch (start us, length us, event | category | flops | bytes accessed | tf_op | source)
XLA Modules:
  0.0 43.4 jit_solution(9642038176161426172)
XLA Ops:
  0.6 41.9 %shard_map.94 = (bf16[1024,128]{1,0:T(8,128)(2,1)S(1)}, bf16[2,512,128]{2,1,0:T(8,128)(2,1)S(1)}) custom-call(bf16[1024,128]{1,0:T(8,128)(2,1)} %bitcast.6, bf16[512,128]{1,0:T(8,128)(2,1)} %k_hbm.1, bf16[512,128]{1,0:T(8,128)(2,1)} %v_hbm.1, bf16[1024,128]{1,0:T(8,128)(2,1)} %bitcast.7, bf16[1024,128]{1,0:T(8,128)(2,1)} %bitcast.8, f32[2,512]{1,0:T(2,128)} %bitcast.9, ...), custom_call_target="tpu_custom_call" | custom-call | tf_op jit(solution)/shard_map/pallas_call | solution.py:462
  42.6 0.8 %shard_map.95 = (bf16[1024,128]{1,0:T(8,128)(2,1)}, bf16[512,128]{1,0:T(8,128)(2,1)}, bf16[512,128]{1,0:T(8,128)(2,1)}) custom-call(bf16[1024,128]{1,0:T(8,128)(2,1)S(1)} %get-tuple-element.8.dq_in, bf16[2,512,128]{2,1,0:T(8,128)(2,1)S(1)} %get-tuple-element.9.dkv_in), custom_call_target="tpu_custom_call" | custom-call | tf_op jit(solution)/shard_map/pallas_call | solution.py:481

commit v5 on v4

v5 whole, which is shorter than its diff:
```python
import functools
import math

import jax
import jax.numpy as jnp
from jax import lax
from jax.experimental import pallas as pl
from jax.experimental.pallas import tpu as pltpu
from jax.sharding import PartitionSpec as P

MESH = pl.DeviceIdType.MESH
SHARDS = 5
KV_CHUNKS = 2
QD_CHUNKS = 4
LOG2E = math.log2(math.e)
NT = (((1,), (1,)), ((), ()))
NN = (((1,), (0,)), ((), ()))


def dot(lhs, rhs, dims):
    return lax.dot_general(lhs, rhs, dims, preferred_element_type=jnp.float32)


def backward_kernel(sizes, q_hbm, k_hbm, v_hbm, o_hbm, do_hbm, lse_hbm, cu_hbm, dq_out, dkv_out,
                    kv_s, kv_w, qd_s, qd_w, ld_s, ld_w, qd_via, ld_via, o_buf, lse_buf, cu_buf, starts, key_t, dq_t, dk_acc, dv_acc, dq_fin, dkv_fin,
                    load_sem, guest_send, guest_recv, fwd_send, fwd_recv, right_send, right_recv, left_send, left_recv, via_recv, back_send, back_recv):
    outer, inner, rows, heads, head = sizes
    group = outer * inner
    pairs = group // 2
    half = pairs // outer
    scale = head ** -0.5
    flat = rows * heads
    k_part = rows // KV_CHUNKS
    lanes = flat // QD_CHUNKS
    span = rows // QD_CHUNKS
    bounds = cu_buf.shape[1]
    rank = lax.axis_index("cpo") * inner + lax.axis_index("cp")

    def resident(pair):
        return (pair + pair // half + 1) % 2

    def host(pair):
        return 2 * pair + resident(pair)

    def helper(pair):
        return (host(pair) + inner) % group

    def visitor(pair):
        return 2 * pair + 1 - resident(pair)

    is_host = rank % 2 == resident(rank // 2)
    is_helper = rank % 2 != resident(rank // 2)
    pair = jnp.where(is_host, rank // 2, ((rank + inner) % group) // 2)
    res = resident(pair)
    gst = 1 - res
    guest = visitor(pair)
    mine = rank // 2
    side = rank % 2
    own = jnp.where(is_host, res, 2)
    prev_res, next_res = resident(pair - 1), resident(pair + 1)
    has_prev, has_prev2 = pair >= 1, pair >= 2
    has_next, has_next2 = pair + 1 < pairs, pair + 2 < pairs
    my_host = host(mine)

    is_carrier = is_helper & (mine == half - 1)
    goes_left1 = is_helper & (mine == half)
    goes_left2 = is_helper & (mine == half + 1)
    before_cut, at_cut, past_cut, past_cut2 = pair == half - 2, pair == half - 1, pair == half, pair == half + 1

    def device(index):
        return (0, index // inner, index % inner)

    def remote(source, target, send, recv, index):
        return pltpu.make_async_remote_copy(src_ref=source, dst_ref=target, send_sem=send, recv_sem=recv,
                                            device_id=device(index), device_id_type=MESH)

    loads = [
        pltpu.make_async_copy(k_hbm, kv_s.at[own, 0], load_sem.at[0]),
        pltpu.make_async_copy(v_hbm, kv_s.at[own, 1], load_sem.at[1]),
        pltpu.make_async_copy(q_hbm, qd_s.at[own, 0], load_sem.at[2]),
        pltpu.make_async_copy(do_hbm, qd_s.at[own, 1], load_sem.at[3]),
        pltpu.make_async_copy(o_hbm, o_buf, load_sem.at[4]),
        pltpu.make_async_copy(lse_hbm, lse_buf, load_sem.at[5]),
        pltpu.make_async_copy(cu_hbm, cu_buf, load_sem.at[6]),
    ]
    for load in loads:
        load.start()

    barrier = pltpu.get_barrier_semaphore()
    for known, peer in (
        (is_host, guest), (is_helper, host(pair)), (is_helper, my_host), (is_helper, (my_host + inner) % group), (is_host, helper(pair)),
        (is_host & has_prev & ~past_cut, host(pair - 1)), (is_host & has_prev2 & ~past_cut & ~past_cut2, host(pair - 2)),
        (is_helper & has_next & ~at_cut, host(pair + 1)), (is_helper & has_next2 & ~at_cut & ~before_cut, host(pair + 2)),
        (is_carrier, host(half - 2)), (is_host & (past_cut | past_cut2), visitor(half - 1)),
        (is_helper & at_cut, visitor(half)), (is_helper & at_cut, visitor(half + 1)),
        (is_helper & before_cut, visitor(half)),
    ):
        @pl.when(known)
        def _():
            pl.semaphore_signal(barrier, inc=1, device_id=device(peer), device_id_type=MESH)

    arrivals = jnp.where(is_host, 2, 3)
    for known, count in (
        (is_host & has_next & ~at_cut, 1), (is_host & has_next2 & ~at_cut & ~before_cut, 1),
        (is_host & has_prev & ~past_cut, 1), (is_host & has_prev2 & ~past_cut & ~past_cut2, 1),
        (is_host & before_cut, 1), (is_carrier, 2), (goes_left1, 2), (goes_left2, 1),
    ):
        arrivals = arrivals + jnp.where(known, count, 0)
    for load in loads:
        load.wait()

    row_id = lax.broadcasted_iota(jnp.int32, (head, heads * head), 0)
    lane_id = lax.broadcasted_iota(jnp.int32, (head, heads * head), 1)
    for part in range(rows // head):
        piece = slice(part * head, (part + 1) * head)
        wide = jnp.zeros((head, heads * head), jnp.float32)
        for g in range(heads):
            column_g = jnp.broadcast_to(lse_buf[g:g + 1, piece], (head, head)).T
            wide = jnp.where(lane_id == row_id * heads + g, jnp.concatenate([column_g] * heads, axis=1), wide)
        ld_s[own, 0:1, part * heads * head:(part + 1) * heads * head] = jnp.sum(wide, axis=0, keepdims=True) * LOG2E
    for part in range(flat // head):
        piece = slice(part * head, (part + 1) * head)
        prod = qd_s[own, 1, piece, :].astype(jnp.float32) * o_buf[piece, :].astype(jnp.float32)
        ld_s[own, 1:2, piece] = jnp.sum(prod.T, axis=0, keepdims=True)

    pl.semaphore_wait(barrier, arrivals)

    def kv_rows(chunk):
        return pl.ds(chunk * k_part, k_part)

    def qd_rows(chunk):
        if isinstance(chunk, int):
            return pl.ds(chunk * lanes, lanes)
        return pl.ds(pl.multiple_of(chunk * lanes, lanes), lanes)

    LD = KV_CHUNKS + QD_CHUNKS

    place = jnp.where(is_host, gst, rank % 2)

    def guest_kv(chunk):
        part = kv_rows(chunk)
        return remote(kv_s.at[2, :, part], kv_s.at[place, :, part], guest_send.at[chunk], guest_recv.at[chunk], my_host)

    def guest_qd(chunk):
        part = qd_rows(chunk)
        return remote(qd_s.at[2, :, part], qd_s.at[place, :, part], guest_send.at[KV_CHUNKS + chunk], guest_recv.at[KV_CHUNKS + chunk], my_host)

    def guest_ld():
        return remote(ld_s.at[2], ld_s.at[place], guest_send.at[LD], guest_recv.at[LD], my_host)

    def fwd_kv(slot, chunk):
        part = kv_rows(chunk)
        return remote(kv_s.at[slot, :, part], kv_s.at[slot, :, part], fwd_send.at[slot, chunk], fwd_recv.at[slot, chunk], helper(pair))

    def fwd_qd(slot, chunk):
        part = qd_rows(chunk)
        return remote(qd_s.at[slot, :, part], qd_s.at[slot, :, part], fwd_send.at[slot, KV_CHUNKS + chunk], fwd_recv.at[slot, KV_CHUNKS + chunk], helper(pair))

    def fwd_ld(slot):
        return remote(ld_s.at[slot], ld_s.at[slot], fwd_send.at[slot, LD], fwd_recv.at[slot, LD], helper(pair))

    def right1(slot, chunk):
        part = kv_rows(chunk)
        to = jnp.where(at_cut, guest, host(pair + 1))
        return remote(kv_s.at[slot, :, part], kv_w.at[slot, :, part], right_send.at[slot, chunk], right_recv.at[slot, chunk], to)

    def right2(chunk):
        part = kv_rows(chunk)
        to = jnp.where(before_cut, visitor(half - 1), host(pair + 2))
        return remote(kv_s.at[1, :, part], kv_w.at[2, :, part], right_send.at[2, chunk], right_recv.at[2, chunk], to)

    def carry1(slot, chunk):
        part = kv_rows(chunk)
        source = kv_s.at[2, :, part] if slot == 1 else kv_w.at[slot, :, part]
        return remote(source, kv_w.at[slot, :, part], right_send.at[slot, chunk], right_recv.at[slot, chunk], host(half))

    def carry2(chunk):
        part = kv_rows(chunk)
        return remote(kv_s.at[2, :, part], kv_w.at[2, :, part], left_send.at[0, chunk], right_recv.at[2, chunk], host(half + 1))

    def left1(slot, chunk, source=None, to=None):
        part = qd_rows(chunk)
        source, to = (slot, helper(pair - 1)) if source is None else (source, to)
        return remote(qd_s.at[source, :, part], qd_w.at[slot, :, part], left_send.at[slot, chunk], left_recv.at[slot, chunk], to)

    def left2(chunk, source=0, to=None):
        part = qd_rows(chunk)
        to = helper(pair - 2) if to is None else to
        return remote(qd_s.at[source, :, part], qd_w.at[2, :, part], left_send.at[2, chunk], left_recv.at[2, chunk], to)

    def left1_ld(slot, source=None, to=None):
        source, to = (slot, helper(pair - 1)) if source is None else (source, to)
        return remote(ld_s.at[source], ld_w.at[slot], left_send.at[slot, QD_CHUNKS], left_recv.at[slot, QD_CHUNKS], to)

    def left2_ld(source=0, to=None):
        to = helper(pair - 2) if to is None else to
        return remote(ld_s.at[source], ld_w.at[2], left_send.at[2, QD_CHUNKS], left_recv.at[2, QD_CHUNKS], to)

    def over_qd(chunk):
        part = qd_rows(chunk)
        return remote(qd_s.at[0, :, part], qd_via.at[:, part], left_send.at[0, chunk], via_recv.at[chunk], visitor(half))

    def over_ld():
        return remote(ld_s.at[0], ld_via, left_send.at[0, QD_CHUNKS], via_recv.at[QD_CHUNKS], visitor(half))

    def relay_qd(chunk):
        part = qd_rows(chunk)
        return remote(qd_via.at[:, part], qd_w.at[2, :, part], left_send.at[0, chunk], left_recv.at[2, chunk], helper(half - 2))

    def relay_qd1(chunk):
        part = qd_rows(chunk)
        return remote(qd_via.at[:, part], qd_w.at[0, :, part], left_send.at[2, chunk], left_recv.at[0, chunk], helper(half - 1))

    def relay_ld1():
        return remote(ld_via, ld_w.at[0], left_send.at[0, QD_CHUNKS], left_recv.at[0, QD_CHUNKS], helper(half - 1))

    def relay_ld2():
        return remote(ld_via, ld_w.at[2], left_send.at[2, QD_CHUNKS], left_recv.at[2, QD_CHUNKS], helper(half - 2))

    def back_dq():
        return remote(dq_fin.at[gst], dq_out, back_send.at[0], back_recv.at[0], guest)

    def back_dkv(slot, part, index, target):
        part_rows = pl.ds(part * (rows // 2), rows // 2)
        return remote(dkv_fin.at[slot, :, part_rows], dkv_out.at[:, part_rows], back_send.at[index + part], back_recv.at[1 + part], target)

    def when(cond, *starts_of):
        @pl.when(cond)
        def _():
            for item in starts_of:
                item().start()

    sends_right1 = is_host & has_next
    sends_right2 = is_host & has_next2 & (res == 1) & ~at_cut
    sends_left1 = is_host & has_prev & ~past_cut
    sends_left2 = is_host & has_prev2 & (res == 0) & ~past_cut & ~past_cut2
    waits_left2 = (pair // half) % 2 == res
    for chunk in range(KV_CHUNKS):
        when(is_helper, lambda: guest_kv(chunk))
        when(sends_right1, lambda: right1(res, chunk))
        when(is_host, lambda: fwd_kv(res, chunk))
        when(sends_right2, lambda: right2(chunk))
    when(is_carrier, *[lambda chunk=chunk: carry1(1, chunk) for chunk in range(KV_CHUNKS)])
    when(is_helper, guest_ld)
    when(is_host, lambda: fwd_ld(res))
    when(sends_left1, lambda: left1_ld(res))
    when(sends_left2, left2_ld)
    for chunk in range(QD_CHUNKS):
        when(is_helper & ~past_cut & ~at_cut, lambda: guest_qd(chunk))
        when(sends_left1, lambda: left1(res, chunk))
        when(is_host, lambda: fwd_qd(res, chunk))
        when(sends_left2 if chunk < QD_CHUNKS // 2 else sends_left2 & ~waits_left2, lambda: left2(chunk))
    when(is_carrier, *[lambda chunk=chunk: carry2(chunk) for chunk in range(KV_CHUNKS)])
    when(is_host & past_cut, over_ld, *[lambda chunk=chunk: over_qd(chunk) for chunk in range(QD_CHUNKS)])

    first = (pair * (2 * rows)).astype(jnp.float32)
    cuts = cu_buf[...].astype(jnp.float32)
    cut_cols = []
    for base in range(0, bounds, head):
        width = min(head, bounds - base)
        row = cuts[:, base:base + width]
        if width < head:
            row = jnp.concatenate([row, jnp.zeros((1, head - width), jnp.float32)], axis=1)
        cut_cols.append(jnp.broadcast_to(row, (head, head)).T - first)
    lane = lax.broadcasted_iota(jnp.int32, (1, head), 1)

    def fill_starts(step, _):
        lane_base = pl.multiple_of((step % (flat // head)) * head, head)
        shard = step // (flat // head)
        token = ((lane + lane_base) // heads + shard * rows).astype(jnp.float32)
        best = jnp.full((head, head), -1e9, jnp.float32)
        for col in cut_cols:
            best = jnp.maximum(best, jnp.where(col <= token, col, -1e9))
        starts[shard, :, pl.ds(lane_base, head)] = jnp.max(best, axis=0, keepdims=True)
        return 0

    lax.fori_loop(0, 2 * (flat // head), fill_starts, 0)

    def directs():
        out = [(goes_left1, left1_ld(side, 2, helper(mine - 1))), (goes_left2, left2_ld(2, helper(mine - 2)))]
        for chunk in range(QD_CHUNKS):
            out.append((goes_left1, left1(side, chunk, 2, helper(mine - 1))))
            out.append((goes_left2, left2(chunk, 2, helper(mine - 2))))
        return out

    @pl.when(goes_left1)
    def _():
        left1_ld(side, 2, helper(mine - 1)).start()
        for chunk in range(QD_CHUNKS):
            left1(side, chunk, 2, helper(mine - 1)).start()

    def scores(kv, key_rows, key_off, qd, ld, part, start, token_off):
        keys, vals = kv[0, key_rows, :], kv[1, key_rows, :]
        qry, dout = qd[0, part, :], qd[1, part, :]
        score = dot(keys, qry, NT)
        grad = dot(vals, dout, NT)
        lse, row_dot = ld[0:1, part], ld[1:2, part]
        key_pos = lax.broadcasted_iota(jnp.int32, score.shape, 0).astype(jnp.float32)
        keep = key_pos >= start[:, part] - key_off
        if token_off is not None:
            token = lax.broadcasted_iota(jnp.int32, (1, lanes), 1) // heads + token_off
            keep = keep & (key_pos <= token.astype(jnp.float32))
        prob = jnp.where(keep, jnp.exp2(score * (scale * LOG2E) - lse), 0.0)
        dsc = (prob * (grad - row_dot)).astype(jnp.bfloat16)
        return prob, dsc, qry, dout

    def q_tile(kv, key_slot, k_from, k_to, key_off, q_slot, chunk, token_off=None):
        part, key_rows = qd_rows(chunk), pl.ds(k_from, k_to - k_from)
        _, dsc, _, _ = scores(kv, key_rows, key_off + k_from, qd_s.at[q_slot], ld_s.at[q_slot], part, starts.at[q_slot], token_off)
        dq_t[q_slot, :, part] += dot(key_t[key_slot, :, k_from:k_to], dsc, NN)

    def k_tile(k_slot, k_from, k_to, qd, ld, q_shard, chunk, token_off=None):
        part, key_rows = qd_rows(chunk), pl.ds(k_from, k_to - k_from)
        key_off = (k_slot * rows + k_from) * 1.0
        prob, dsc, qry, dout = scores(kv_s.at[k_slot], key_rows, key_off, qd, ld, part, starts.at[q_shard], token_off)
        dv_acc[k_slot, key_rows, :] += dot(prob.astype(jnp.bfloat16), dout, NN)
        dk_acc[k_slot, key_rows, :] += dot(dsc, qry, NN)

    def finish_dq(slot, target):
        for part in range(flat // head):
            piece = slice(part * head, (part + 1) * head)
            target[piece, :] = (scale * dq_t[slot, :, piece].T).astype(jnp.bfloat16)

    def finish_dkv(slot, part):
        part_rows = slice(part * (rows // 2), (part + 1) * (rows // 2))
        dkv_fin[slot, 0, part_rows, :] = (scale * dk_acc[slot, part_rows, :]).astype(jnp.bfloat16)
        dkv_fin[slot, 1, part_rows, :] = dv_acc[slot, part_rows, :].astype(jnp.bfloat16)

    @pl.when(is_host)
    def _():
        dq_t[...] = jnp.zeros_like(dq_t)

        relays_right1 = has_next & ~at_cut
        relays_right2 = has_next2 & (gst == 1) & ~at_cut
        relays_left1 = has_prev & ~past_cut
        relays_left2 = has_prev2 & (gst == 0) & ~past_cut & ~past_cut2

        def diagonal(slot, chunk):
            q_tile(kv_s.at[slot], slot, 0, (chunk + 1) * span, slot * rows * 1.0, slot, chunk, chunk * span)

        key_t[res] = kv_s[res, 0, :, :].T
        for chunk in range(QD_CHUNKS):
            diagonal(res, chunk)
        for chunk in range(KV_CHUNKS):
            guest_kv(chunk).wait_recv()
            fwd_kv(gst, chunk).start()
            when(relays_right2, lambda: right2(chunk))
            when(relays_right1 & ~has_prev, lambda: right1(gst, chunk))
        guest_ld().wait_recv()
        fwd_ld(gst).start()
        when(relays_left1, lambda: left1_ld(gst))
        when(relays_left2, left2_ld)
        key_t[gst] = kv_s[gst, 0, :, :].T
        soon = jnp.where(past_cut, 1 - prev_res, prev_res)
        prev_off = (soon - 2) * rows * 1.0
        late_off = (-1 - soon) * rows * 1.0

        def early_keys():
            for chunk in range(KV_CHUNKS):
                right1(soon, chunk).wait_recv()
            key_t[2] = kv_w[soon, 0, :, :].T

        def early_tiles(chunk):
            q_tile(kv_w.at[soon], 2, 0, rows, prev_off, res, chunk)
            q_tile(kv_w.at[soon], 2, 0, rows, prev_off, gst, chunk)

        for chunk in range(QD_CHUNKS):
            guest_qd(chunk).wait_recv()
            when(relays_left1 & has_next, lambda: left1(gst, chunk))
            fwd_qd(gst, chunk).start()
            when(relays_left2 & ~waits_left2, lambda: left2(chunk))
            diagonal(gst, chunk)
            q_tile(kv_s.at[0], 0, 0, rows, 0.0, 1, chunk)

            @pl.when(has_prev & ~past_cut)
            def _():
                if chunk == 0:
                    early_keys()
                early_tiles(chunk)

        for chunk in range(KV_CHUNKS):
            when(relays_right1 & has_prev, lambda: right1(gst, chunk))
        @pl.when(past_cut)
        def _():
            early_keys()

            def both(chunk, _):
                early_tiles(chunk)
                return 0

            lax.fori_loop(0, QD_CHUNKS, both, 0)

        for chunk in range(QD_CHUNKS):
            when((relays_left2 | sends_left2 if chunk >= QD_CHUNKS // 2 else relays_left2) & waits_left2, lambda: left2(chunk))

        def far_keys():
            for chunk in range(KV_CHUNKS):
                right2(chunk).wait_recv()
            key_t[2] = kv_w[2, 0, :, :].T
            for chunk in range(QD_CHUNKS):
                q_tile(kv_w.at[2], 2, chunk * span, rows, -3.0 * rows, 0, chunk)

        @pl.when(has_prev2 & ~past_cut)
        def _():
            far_keys()

        for chunk in range(QD_CHUNKS):
            when(relays_left1 & ~has_next, lambda: left1(gst, chunk))

        def late_keys(slot, part, step):
            @pl.when(has_prev)
            def _():
                for index in range(2):
                    q_tile(kv_w.at[1 - soon], 2, part * k_part, (part + 1) * k_part, late_off, slot, 2 * step + index)

        for chunk in range(KV_CHUNKS):
            @pl.when(has_prev)
            def _():
                right1(1 - soon, chunk).wait_recv()
                key_t[2, :, chunk * k_part:(chunk + 1) * k_part] = kv_w[1 - soon, 0, chunk * k_part:(chunk + 1) * k_part, :].T

            late_keys(gst, chunk, 0)
            late_keys(gst, chunk, 1)
            if chunk == KV_CHUNKS - 1:
                finish_dq(gst, dq_fin.at[gst])
            late_keys(res, chunk, 0)
            if chunk == KV_CHUNKS - 1:
                back_dq().start()
            late_keys(res, chunk, 1)

        @pl.when(past_cut)
        def _():
            far_keys()

        finish_dq(res, dq_out)

        for chunk in range(KV_CHUNKS):
            fwd_kv(res, chunk).wait_send()
            fwd_kv(gst, chunk).wait_send()
        for chunk in range(QD_CHUNKS):
            fwd_qd(res, chunk).wait_send()
            fwd_qd(gst, chunk).wait_send()
        fwd_ld(res).wait_send()
        fwd_ld(gst).wait_send()

        @pl.when(has_next)
        def _():
            for chunk in range(KV_CHUNKS):
                right1(res, chunk).wait_send()

        @pl.when(relays_right1)
        def _():
            for chunk in range(KV_CHUNKS):
                right1(gst, chunk).wait_send()

        @pl.when(sends_right2 | relays_right2)
        def _():
            for chunk in range(KV_CHUNKS):
                right2(chunk).wait_send()

        @pl.when(sends_left1)
        def _():
            for slot in range(2):
                for chunk in range(QD_CHUNKS):
                    left1(slot, chunk).wait_send()
                left1_ld(slot).wait_send()

        @pl.when(past_cut)
        def _():
            over_ld().wait_send()
            for chunk in range(QD_CHUNKS):
                over_qd(chunk).wait_send()

        @pl.when(sends_left2 | relays_left2)
        def _():
            for chunk in range(QD_CHUNKS):
                left2(chunk).wait_send()
            left2_ld().wait_send()

        back_dq().wait_send()
        for part in range(2):
            back_dkv(0, part, 1, guest).wait_recv()

    @pl.when(is_helper)
    def _():
        lax.fori_loop(2 * (flat // head), SHARDS * (flat // head), fill_starts, 0)
        dk_acc[...] = jnp.zeros_like(dk_acc)
        dv_acc[...] = jnp.zeros_like(dv_acc)

        def diagonal(slot, chunk):
            k_tile(slot, 0, (chunk + 1) * span, qd_s.at[slot], ld_s.at[slot], slot, chunk, chunk * span)

        def carry(slot):
            @pl.when(is_carrier)
            def _():
                for chunk in range(KV_CHUNKS):
                    carry1(slot, chunk).wait_recv()
                    carry1(slot, chunk).start()

        carry(0)
        for chunk in range(KV_CHUNKS):
            fwd_kv(res, chunk).wait_recv()
        fwd_ld(res).wait_recv()
        for chunk in range(QD_CHUNKS):
            fwd_qd(res, chunk).wait_recv()
            diagonal(res, chunk)
        for chunk in range(QD_CHUNKS):
            when(past_cut | at_cut, lambda: guest_qd(chunk))
        carry(2)
        for chunk in range(KV_CHUNKS):
            fwd_kv(gst, chunk).wait_recv()
        fwd_ld(gst).wait_recv()

        def next_queries(slot, chunk):
            left1(slot, chunk).wait_recv()
            k_tile(res, 0, rows, qd_w.at[slot], ld_w.at[slot], slot + 2, chunk)
            k_tile(gst, 0, rows, qd_w.at[slot], ld_w.at[slot], slot + 2, chunk)

        soon_next = jnp.where(at_cut, 1 - next_res, next_res)

        @pl.when(has_next & ~at_cut)
        def _():
            left1_ld(soon_next).wait_recv()

        @pl.when(goes_left1)
        def _():
            over_ld().wait_recv()
            relay_ld1().start()
            relay_ld2().start()
            for chunk in range(QD_CHUNKS):
                over_qd(chunk).wait_recv()
                relay_qd1(chunk).start()
                relay_qd(chunk).start()

        for chunk in range(QD_CHUNKS):
            @pl.when(has_next & ~at_cut)
            def _():
                next_queries(soon_next, chunk)

            fwd_qd(gst, chunk).wait_recv()
            diagonal(gst, chunk)
            k_tile(0, 0, rows, qd_s.at[1], ld_s.at[1], 1, chunk)
            if chunk == 0:
                @pl.when(goes_left2)
                def _():
                    left2_ld(2, helper(mine - 2)).start()
                    for far in range(QD_CHUNKS):
                        left2(far, 2, helper(mine - 2)).start()

        def all_queries(slot):
            left1_ld(slot).wait_recv()

            def one(chunk, _):
                next_queries(slot, chunk)
                return 0

            lax.fori_loop(0, QD_CHUNKS, one, 0)

        @pl.when(at_cut)
        def _():
            all_queries(soon_next)

        @pl.when(has_next)
        def _():
            all_queries(1 - soon_next)


        @pl.when(gst == 0)
        def _():
            finish_dkv(0, 0)
            finish_dkv(0, 1)

        for part in range(2):
            @pl.when(has_next2)
            def _():
                if part == 0:
                    left2_ld().wait_recv()
                for chunk in range(part * QD_CHUNKS // 2, (part + 1) * QD_CHUNKS // 2):
                    left2(chunk).wait_recv()
                    k_tile(1, chunk * span, rows, qd_w.at[2], ld_w.at[2], 4, chunk)

            finish_dkv(1, part)

            @pl.when(gst == 1)
            def _():
                finish_dkv(0, part)
                back_dkv(1, part, 1, guest).start()
                back_dkv(0, part, 3, host(pair)).start()

            @pl.when(gst == 0)
            def _():
                if part == 0:
                    back_dkv(0, 0, 1, guest).start()
                    back_dkv(0, 1, 1, guest).start()
                back_dkv(1, part, 3, host(pair)).start()

        @pl.when(goes_left1)
        def _():
            relay_ld1().wait_send()
            relay_ld2().wait_send()
            for chunk in range(QD_CHUNKS):
                relay_qd1(chunk).wait_send()
                relay_qd(chunk).wait_send()

        @pl.when(is_carrier)
        def _():
            for chunk in range(KV_CHUNKS):
                for slot in range(3):
                    carry1(slot, chunk).wait_send()
                carry2(chunk).wait_send()

        for chunk in range(KV_CHUNKS):
            guest_kv(chunk).wait_send()
        for chunk in range(QD_CHUNKS):
            guest_qd(chunk).wait_send()
        guest_ld().wait_send()
        for cond, copy in directs():
            @pl.when(cond)
            def _():
                copy.wait_send()

        for part in range(2):
            back_dkv(gst, part, 1, guest).wait_send()
            back_dkv(res, part, 3, host(pair)).wait_send()
            back_dkv(0, part, 1, guest).wait_recv()
        back_dq().wait_recv()


def store_kernel(dq_in, dkv_in, dq_hbm, dk_hbm, dv_hbm, sem):
    copies = [pltpu.make_async_copy(source, target, sem.at[index])
              for index, (source, target) in enumerate(((dq_in, dq_hbm), (dkv_in.at[0], dk_hbm), (dkv_in.at[1], dv_hbm)))]
    for copy in copies:
        copy.start()
    for copy in copies:
        copy.wait()


def solution(mesh):
    outer, inner = mesh.shape["cpo"], mesh.shape["cp"]

    def local(queries, keys, values, attn_out, logsumexp, d_out, cu_seqlens):
        rows, heads, head = queries.shape
        flat = rows * heads
        low, full = jnp.bfloat16, jnp.float32
        any_spec = pl.BlockSpec(memory_space=pl.ANY)
        vmem_spec = pl.BlockSpec(memory_space=pltpu.VMEM)
        dma = pltpu.SemaphoreType.DMA
        moves = KV_CHUNKS + QD_CHUNKS + 1
        grads = pl.pallas_call(
            functools.partial(backward_kernel, (outer, inner, rows, heads, head)),
            out_shape=(pltpu.VMEM((flat, head), low), pltpu.VMEM((2, rows, head), low)),
            in_specs=[any_spec] * 7,
            out_specs=(vmem_spec,) * 2,
            scratch_shapes=[
                pltpu.VMEM((3, 2, rows, head), low), pltpu.VMEM((3, 2, rows, head), low),
                pltpu.VMEM((3, 2, flat, head), low), pltpu.VMEM((3, 2, flat, head), low),
                pltpu.VMEM((3, 2, flat), full), pltpu.VMEM((3, 2, flat), full), pltpu.VMEM((2, flat, head), low), pltpu.VMEM((2, flat), full),
                pltpu.VMEM((flat, head), low), pltpu.VMEM((heads, rows), full), pltpu.VMEM((1, cu_seqlens.shape[0]), jnp.int32),
                pltpu.VMEM((SHARDS, 1, flat), full), pltpu.VMEM((3, head, rows), low),
                pltpu.VMEM((2, head, flat), full), pltpu.VMEM((2, rows, head), full), pltpu.VMEM((2, rows, head), full),
                pltpu.VMEM((2, flat, head), low), pltpu.VMEM((2, 2, rows, head), low),
                dma((7,)), dma((moves,)), dma((moves,)), dma((2, moves)), dma((2, moves)),
                dma((3, KV_CHUNKS)), dma((3, KV_CHUNKS)), dma((3, QD_CHUNKS + 1)), dma((3, QD_CHUNKS + 1)), dma((QD_CHUNKS + 1,)), dma((5,)), dma((3,)),
            ],
            compiler_params=pltpu.CompilerParams(collective_id=0, has_side_effects=True),
        )(queries.reshape(flat, head), keys, values, attn_out.reshape(flat, head), d_out.reshape(flat, head),
          logsumexp.T, cu_seqlens.reshape(1, -1))
        d_query, d_key, d_value = pl.pallas_call(
            store_kernel,
            out_shape=(jax.ShapeDtypeStruct((flat, head), low), jax.ShapeDtypeStruct((rows, head), low), jax.ShapeDtypeStruct((rows, head), low)),
            in_specs=[vmem_spec] * 2, out_specs=(any_spec,) * 3, scratch_shapes=[dma((3,))],
        )(*(pltpu.with_memory_space_constraint(grad, pltpu.VMEM) for grad in grads))
        return d_query.reshape(rows, heads, head), d_key, d_value

    seq_spec = P(("dp", "cpo", "cp"))
    return jax.shard_map(local, mesh=mesh, in_specs=(seq_spec,) * 6 + (P("dp"),), out_specs=(seq_spec,) * 3, check_vma=False)
```

time: 43.5 us -> 35.2 us (0.81)
  the two profiles are of different devices: /device:TPU:126 before, /device:TPU:123 now
where the time goes in v5:
time: 35.2 us; the launch traced here: 35.1 us
  Pallas kernels  34.3 us (97%)
  between operations  0.82 us (2%)
    pallas_call x1, Pallas kernels, local(): pl.pallas_call(functools.partial(backward_kernel, (outer, inner, rows, he...  33.5 us
    pallas_call x1, Pallas kernels, local(): pl.pallas_call(store_kernel, out_shape=(jax.ShapeDtypeStruct((flat, head)...  0.81 us

profile of v5, /device:TPU:123, one launch (start us, length us, event | category | flops | bytes accessed | tf_op | source)
XLA Modules:
  0.0 35.1 jit_solution(12019780119493280214)
XLA Ops:
  0.6 33.5 %shard_map.94 = (bf16[1024,128]{1,0:T(8,128)(2,1)S(1)}, bf16[2,512,128]{2,1,0:T(8,128)(2,1)S(1)}) custom-call(bf16[1024,128]{1,0:T(8,128)(2,1)} %bitcast.6, bf16[512,128]{1,0:T(8,128)(2,1)} %k_hbm.1, bf16[512,128]{1,0:T(8,128)(2,1)} %v_hbm.1, bf16[1024,128]{1,0:T(8,128)(2,1)} %bitcast.7, bf16[1024,128]{1,0:T(8,128)(2,1)} %bitcast.8, f32[2,512]{1,0:T(2,128)} %bitcast.9, ...), custom_call_target="tpu_custom_call" | custom-call | tf_op jit(solution)/shard_map/pallas_call | solution.py:649
  34.1 0.8 %shard_map.95 = (bf16[1024,128]{1,0:T(8,128)(2,1)}, bf16[512,128]{1,0:T(8,128)(2,1)}, bf16[512,128]{1,0:T(8,128)(2,1)}) custom-call(bf16[1024,128]{1,0:T(8,128)(2,1)S(1)} %get-tuple-element.8.dq_in, bf16[2,512,128]{2,1,0:T(8,128)(2,1)S(1)} %get-tuple-element.9.dkv_in), custom_call_target="tpu_custom_call" | custom-call | tf_op jit(solution)/shard_map/pallas_call | solution.py:668

commit v6 on v5

--- a/solution.py
+++ b/solution.py
@@ -109,6 +109,125 @@
     for load in loads:
         load.wait()
 
+    pl.semaphore_wait(barrier, arrivals)
+
+    def kv_rows(chunk):
+        return pl.ds(chunk * k_part, k_part)
+
+    def qd_rows(chunk):
+        if isinstance(chunk, int):
+            return pl.ds(chunk * lanes, lanes)
+        return pl.ds(pl.multiple_of(chunk * lanes, lanes), lanes)
+
+    LD = KV_CHUNKS + QD_CHUNKS
+
+    place = jnp.where(is_host, gst, rank % 2)
+
+    def guest_kv(chunk):
+        part = kv_rows(chunk)
+        return remote(kv_s.at[2, :, part], kv_s.at[place, :, part], guest_send.at[chunk], guest_recv.at[chunk], my_host)
+
+    def guest_qd(chunk):
+        part = qd_rows(chunk)
+        return remote(qd_s.at[2, :, part], qd_s.at[place, :, part], guest_send.at[KV_CHUNKS + chunk], guest_recv.at[KV_CHUNKS + chunk], my_host)
+
+    def guest_ld():
+        return remote(ld_s.at[2], ld_s.at[place], guest_send.at[LD], guest_recv.at[LD], my_host)
+
+    def fwd_kv(slot, chunk):
+        part = kv_rows(chunk)
+        return remote(kv_s.at[slot, :, part], kv_s.at[slot, :, part], fwd_send.at[slot, chunk], fwd_recv.at[slot, chunk], helper(pair))
+
+    def fwd_qd(slot, chunk):
+        part = qd_rows(chunk)
+        return remote(qd_s.at[slot, :, part], qd_s.at[slot, :, part], fwd_send.at[slot, KV_CHUNKS + chunk], fwd_recv.at[slot, KV_CHUNKS + chunk], helper(pair))
+
+    def fwd_ld(slot):
+        return remote(ld_s.at[slot], ld_s.at[slot], fwd_send.at[slot, LD], fwd_recv.at[slot, LD], helper(pair))
+
+    def right1(slot, chunk):
+        part = kv_rows(chunk)
+        to = jnp.where(at_cut, guest, host(pair + 1))
+        return remote(kv_s.at[slot, :, part], kv_w.at[slot, :, part], right_send.at[slot, chunk], right_recv.at[slot, chunk], to)
+
+    def right2(chunk):
+        part = kv_rows(chunk)
+        to = jnp.where(before_cut, visitor(half - 1), host(pair + 2))
+        return remote(kv_s.at[1, :, part], kv_w.at[2, :, part], right_send.at[2, chunk], right_recv.at[2, chunk], to)
+
+    def carry1(slot, chunk):
+        part = kv_rows(chunk)
+        source = kv_s.at[2, :, part] if slot == 1 else kv_w.at[slot, :, part]
+        return remote(source, kv_w.at[slot, :, part], right_send.at[slot, chunk], right_recv.at[slot, chunk], host(half))
+
+    def carry2(chunk):
+        part = kv_rows(chunk)
+        return remote(kv_s.at[2, :, part], kv_w.at[2, :, part], left_send.at[0, chunk], right_recv.at[2, chunk], host(half + 1))
+
+    def left1(slot, chunk, source=None, to=None):
+        part = qd_rows(chunk)
+        source, to = (slot, helper(pair - 1)) if source is None else (source, to)
+        return remote(qd_s.at[source, :, part], qd_w.at[slot, :, part], left_send.at[slot, chunk], left_recv.at[slot, chunk], to)
+
+    def left2(chunk, source=0, to=None):
+        part = qd_rows(chunk)
+        to = helper(pair - 2) if to is None else to
+        return remote(qd_s.at[source, :, part], qd_w.at[2, :, part], left_send.at[2, chunk], left_recv.at[2, chunk], to)
+
+    def left1_ld(slot, source=None, to=None):
+        source, to = (slot, helper(pair - 1)) if source is None else (source, to)
+        return remote(ld_s.at[source], ld_w.at[slot], left_send.at[slot, QD_CHUNKS], left_recv.at[slot, QD_CHUNKS], to)
+
+    def left2_ld(source=0, to=None):
+        to = helper(pair - 2) if to is None else to
+        return remote(ld_s.at[source], ld_w.at[2], left_send.at[2, QD_CHUNKS], left_recv.at[2, QD_CHUNKS], to)
+
+    def over_qd(chunk):
+        part = qd_rows(chunk)
+        return remote(qd_s.at[0, :, part], qd_via.at[:, part], left_send.at[0, chunk], via_recv.at[chunk], visitor(half))
+
+    def over_ld():
+        return remote(ld_s.at[0], ld_via, left_send.at[0, QD_CHUNKS], via_recv.at[QD_CHUNKS], visitor(half))
+
+    def relay_qd(chunk):
+        part = qd_rows(chunk)
+        return remote(qd_via.at[:, part], qd_w.at[2, :, part], left_send.at[0, chunk], left_recv.at[2, chunk], helper(half - 2))
+
+    def relay_qd1(chunk):
+        part = qd_rows(chunk)
+        return remote(qd_via.at[:, part], qd_w.at[0, :, part], left_send.at[2, chunk], left_recv.at[0, chunk], helper(half - 1))
+
+    def relay_ld1():
+        return remote(ld_via, ld_w.at[0], left_send.at[0, QD_CHUNKS], left_recv.at[0, QD_CHUNKS], helper(half - 1))
+
+    def relay_ld2():
+        return remote(ld_via, ld_w.at[2], left_send.at[2, QD_CHUNKS], left_recv.at[2, QD_CHUNKS], helper(half - 2))
+
+    def back_dq(part):
+        part_rows = pl.ds(part * (flat // 2), flat // 2)
+        return remote(dq_fin.at[gst, part_rows], dq_out.at[part_rows], back_send.at[5 * part], back_recv.at[3 * part], guest)
+
+    def back_dkv(slot, part, index, target):
+        part_rows = pl.ds(part * (rows // 2), rows // 2)
+        return remote(dkv_fin.at[slot, :, part_rows], dkv_out.at[:, part_rows], back_send.at[index + part], back_recv.at[1 + part], target)
+
+    def when(cond, *starts_of):
+        @pl.when(cond)
+        def _():
+            for item in starts_of:
+                item().start()
+
+    sends_right1 = is_host & has_next
+    sends_right2 = is_host & has_next2 & (res == 1) & ~at_cut
+    sends_left1 = is_host & has_prev & ~past_cut
+    sends_left2 = is_host & has_prev2 & (res == 0) & ~past_cut & ~past_cut2
+    waits_left2 = (pair // half) % 2 == res
+    for chunk in range(KV_CHUNKS):
+        when(is_helper, lambda: guest_kv(chunk))
+        when(sends_right1, lambda: right1(res, chunk))
+        when(is_host, lambda: fwd_kv(res, chunk))
+        when(sends_right2, lambda: right2(chunk))
+    when(is_carrier, *[lambda chunk=chunk: carry1(1, chunk) for chunk in range(KV_CHUNKS)])
     row_id = lax.broadcasted_iota(jnp.int32, (head, heads * head), 0)
     lane_id = lax.broadcasted_iota(jnp.int32, (head, heads * head), 1)
     for part in range(rows // head):
@@ -123,124 +242,6 @@
         prod = qd_s[own, 1, piece, :].astype(jnp.float32) * o_buf[piece, :].astype(jnp.float32)
         ld_s[own, 1:2, piece] = jnp.sum(prod.T, axis=0, keepdims=True)
 
-    pl.semaphore_wait(barrier, arrivals)
-
-    def kv_rows(chunk):
-        return pl.ds(chunk * k_part, k_part)
-
-    def qd_rows(chunk):
-        if isinstance(chunk, int):
-            return pl.ds(chunk * lanes, lanes)
-        return pl.ds(pl.multiple_of(chunk * lanes, lanes), lanes)
-
-    LD = KV_CHUNKS + QD_CHUNKS
-
-    place = jnp.where(is_host, gst, rank % 2)
-
-    def guest_kv(chunk):
-        part = kv_rows(chunk)
-        return remote(kv_s.at[2, :, part], kv_s.at[place, :, part], guest_send.at[chunk], guest_recv.at[chunk], my_host)
-
-    def guest_qd(chunk):
-        part = qd_rows(chunk)
-        return remote(qd_s.at[2, :, part], qd_s.at[place, :, part], guest_send.at[KV_CHUNKS + chunk], guest_recv.at[KV_CHUNKS + chunk], my_host)
-
-    def guest_ld():
-        return remote(ld_s.at[2], ld_s.at[place], guest_send.at[LD], guest_recv.at[LD], my_host)
-
-    def fwd_kv(slot, chunk):
-        part = kv_rows(chunk)
-        return remote(kv_s.at[slot, :, part], kv_s.at[slot, :, part], fwd_send.at[slot, chunk], fwd_recv.at[slot, chunk], helper(pair))
-
-    def fwd_qd(slot, chunk):
-        part = qd_rows(chunk)
-        return remote(qd_s.at[slot, :, part], qd_s.at[slot, :, part], fwd_send.at[slot, KV_CHUNKS + chunk], fwd_recv.at[slot, KV_CHUNKS + chunk], helper(pair))
-
-    def fwd_ld(slot):
-        return remote(ld_s.at[slot], ld_s.at[slot], fwd_send.at[slot, LD], fwd_recv.at[slot, LD], helper(pair))
-
-    def right1(slot, chunk):
-        part = kv_rows(chunk)
-        to = jnp.where(at_cut, guest, host(pair + 1))
-        return remote(kv_s.at[slot, :, part], kv_w.at[slot, :, part], right_send.at[slot, chunk], right_recv.at[slot, chunk], to)
-
-    def right2(chunk):
-        part = kv_rows(chunk)
-        to = jnp.where(before_cut, visitor(half - 1), host(pair + 2))
-        return remote(kv_s.at[1, :, part], kv_w.at[2, :, part], right_send.at[2, chunk], right_recv.at[2, chunk], to)
-
-    def carry1(slot, chunk):
-        part = kv_rows(chunk)
-        source = kv_s.at[2, :, part] if slot == 1 else kv_w.at[slot, :, part]
-        return remote(source, kv_w.at[slot, :, part], right_send.at[slot, chunk], right_recv.at[slot, chunk], host(half))
-
-    def carry2(chunk):
-        part = kv_rows(chunk)
-        return remote(kv_s.at[2, :, part], kv_w.at[2, :, part], left_send.at[0, chunk], right_recv.at[2, chunk], host(half + 1))
-
-    def left1(slot, chunk, source=None, to=None):
-        part = qd_rows(chunk)
-        source, to = (slot, helper(pair - 1)) if source is None else (source, to)
-        return remote(qd_s.at[source, :, part], qd_w.at[slot, :, part], left_send.at[slot, chunk], left_recv.at[slot, chunk], to)
-
-    def left2(chunk, source=0, to=None):
-        part = qd_rows(chunk)
-        to = helper(pair - 2) if to is None else to
-        return remote(qd_s.at[source, :, part], qd_w.at[2, :, part], left_send.at[2, chunk], left_recv.at[2, chunk], to)
-
-    def left1_ld(slot, source=None, to=None):
-        source, to = (slot, helper(pair - 1)) if source is None else (source, to)
-        return remote(ld_s.at[source], ld_w.at[slot], left_send.at[slot, QD_CHUNKS], left_recv.at[slot, QD_CHUNKS], to)
-
-    def left2_ld(source=0, to=None):
-        to = helper(pair - 2) if to is None else to
-        return remote(ld_s.at[source], ld_w.at[2], left_send.at[2, QD_CHUNKS], left_recv.at[2, QD_CHUNKS], to)
-
-    def over_qd(chunk):
-        part = qd_rows(chunk)
-        return remote(qd_s.at[0, :, part], qd_via.at[:, part], left_send.at[0, chunk], via_recv.at[chunk], visitor(half))
-
-    def over_ld():
-        return remote(ld_s.at[0], ld_via, left_send.at[0, QD_CHUNKS], via_recv.at[QD_CHUNKS], visitor(half))
-
-    def relay_qd(chunk):
-        part = qd_rows(chunk)
-        return remote(qd_via.at[:, part], qd_w.at[2, :, part], left_send.at[0, chunk], left_recv.at[2, chunk], helper(half - 2))
-
-    def relay_qd1(chunk):
-        part = qd_rows(chunk)
-        return remote(qd_via.at[:, part], qd_w.at[0, :, part], left_send.at[2, chunk], left_recv.at[0, chunk], helper(half - 1))
-
-    def relay_ld1():
-        return remote(ld_via, ld_w.at[0], left_send.at[0, QD_CHUNKS], left_recv.at[0, QD_CHUNKS], helper(half - 1))
-
-    def relay_ld2():
-        return remote(ld_via, ld_w.at[2], left_send.at[2, QD_CHUNKS], left_recv.at[2, QD_CHUNKS], helper(half - 2))
-
-    def back_dq():
-        return remote(dq_fin.at[gst], dq_out, back_send.at[0], back_recv.at[0], guest)
-
-    def back_dkv(slot, part, index, target):
-        part_rows = pl.ds(part * (rows // 2), rows // 2)
-        return remote(dkv_fin.at[slot, :, part_rows], dkv_out.at[:, part_rows], back_send.at[index + part], back_recv.at[1 + part], target)
-
-    def when(cond, *starts_of):
-        @pl.when(cond)
-        def _():
-            for item in starts_of:
-                item().start()
-
-    sends_right1 = is_host & has_next
-    sends_right2 = is_host & has_next2 & (res == 1) & ~at_cut
-    sends_left1 = is_host & has_prev & ~past_cut
-    sends_left2 = is_host & has_prev2 & (res == 0) & ~past_cut & ~past_cut2
-    waits_left2 = (pair // half) % 2 == res
-    for chunk in range(KV_CHUNKS):
-        when(is_helper, lambda: guest_kv(chunk))
-        when(sends_right1, lambda: right1(res, chunk))
-        when(is_host, lambda: fwd_kv(res, chunk))
-        when(sends_right2, lambda: right2(chunk))
-    when(is_carrier, *[lambda chunk=chunk: carry1(1, chunk) for chunk in range(KV_CHUNKS)])
     when(is_helper, guest_ld)
     when(is_host, lambda: fwd_ld(res))
     when(sends_left1, lambda: left1_ld(res))
@@ -316,8 +317,8 @@
         dv_acc[k_slot, key_rows, :] += dot(prob.astype(jnp.bfloat16), dout, NN)
         dk_acc[k_slot, key_rows, :] += dot(dsc, qry, NN)
 
-    def finish_dq(slot, target):
-        for part in range(flat // head):
+    def finish_dq(slot, target, half_rows):
+        for part in range(half_rows * flat // head // 2, (half_rows + 1) * flat // head // 2):
             piece = slice(part * head, (part + 1) * head)
             target[piece, :] = (scale * dq_t[slot, :, piece].T).astype(jnp.bfloat16)
 
@@ -345,7 +346,7 @@
             guest_kv(chunk).wait_recv()
             fwd_kv(gst, chunk).start()
             when(relays_right2, lambda: right2(chunk))
-            when(relays_right1 & ~has_prev, lambda: right1(gst, chunk))
+            when(relays_right1, lambda: right1(gst, chunk))
         guest_ld().wait_recv()
         fwd_ld(gst).start()
         when(relays_left1, lambda: left1_ld(gst))
@@ -369,6 +370,9 @@
             when(relays_left1 & has_next, lambda: left1(gst, chunk))
             fwd_qd(gst, chunk).start()
             when(relays_left2 & ~waits_left2, lambda: left2(chunk))
+            if chunk >= QD_CHUNKS // 2:
+                when(relays_left2 & waits_left2, lambda: left2(chunk - QD_CHUNKS // 2))
+                when(sends_left2 & waits_left2, lambda: left2(chunk))
             diagonal(gst, chunk)
             q_tile(kv_s.at[0], 0, 0, rows, 0.0, 1, chunk)
 
@@ -378,8 +382,8 @@
                     early_keys()
                 early_tiles(chunk)
 
-        for chunk in range(KV_CHUNKS):
-            when(relays_right1 & has_prev, lambda: right1(gst, chunk))
+        for chunk in range(QD_CHUNKS // 2):
+            when(relays_left1 & ~has_next, lambda: left1(gst, chunk))
         @pl.when(past_cut)
         def _():
             early_keys()
@@ -390,8 +394,8 @@
 
             lax.fori_loop(0, QD_CHUNKS, both, 0)
 
-        for chunk in range(QD_CHUNKS):
-            when((relays_left2 | sends_left2 if chunk >= QD_CHUNKS // 2 else relays_left2) & waits_left2, lambda: left2(chunk))
+        for chunk in range(QD_CHUNKS // 2, QD_CHUNKS):
+            when(relays_left2 & waits_left2, lambda: left2(chunk))
 
         def far_keys():
             for chunk in range(KV_CHUNKS):
@@ -404,7 +408,7 @@
         def _():
             far_keys()
 
-        for chunk in range(QD_CHUNKS):
+        for chunk in range(QD_CHUNKS // 2, QD_CHUNKS):
             when(relays_left1 & ~has_next, lambda: left1(gst, chunk))
 
         def late_keys(slot, part, step):
@@ -419,20 +423,25 @@
                 right1(1 - soon, chunk).wait_recv()
                 key_t[2, :, chunk * k_part:(chunk + 1) * k_part] = kv_w[1 - soon, 0, chunk * k_part:(chunk + 1) * k_part, :].T
 
+            last = chunk == KV_CHUNKS - 1
             late_keys(gst, chunk, 0)
+            if last:
+                finish_dq(gst, dq_fin.at[gst], 0)
             late_keys(gst, chunk, 1)
-            if chunk == KV_CHUNKS - 1:
-                finish_dq(gst, dq_fin.at[gst])
+            if last:
+                back_dq(0).start()
+                finish_dq(gst, dq_fin.at[gst], 1)
             late_keys(res, chunk, 0)
-            if chunk == KV_CHUNKS - 1:
-                back_dq().start()
+            if last:
+                back_dq(1).start()
             late_keys(res, chunk, 1)
 
         @pl.when(past_cut)
         def _():
             far_keys()
 
-        finish_dq(res, dq_out)
+        finish_dq(res, dq_out, 0)
+        finish_dq(res, dq_out, 1)
 
         for chunk in range(KV_CHUNKS):
             fwd_kv(res, chunk).wait_send()
@@ -477,7 +486,8 @@
                 left2(chunk).wait_send()
             left2_ld().wait_send()
 
-        back_dq().wait_send()
+        back_dq(0).wait_send()
+        back_dq(1).wait_send()
         for part in range(2):
             back_dkv(0, part, 1, guest).wait_recv()
 
@@ -560,14 +570,33 @@
         def _():
             all_queries(soon_next)
 
-        @pl.when(has_next)
-        def _():
-            all_queries(1 - soon_next)
+        late = 1 - soon_next
+        is_early = has_next & (gst == 0)
+
+        @pl.when(is_early)
+        def _():
+            left1_ld(late).wait_recv()
+            for chunk in range(QD_CHUNKS):
+                left1(late, chunk).wait_recv()
+                k_tile(0, chunk * span, rows, qd_w.at[1], ld_w.at[1], 3, chunk)
+                if chunk == QD_CHUNKS // 2 - 1:
+                    finish_dkv(0, 0)
+                k_tile(1, 0, rows, qd_w.at[1], ld_w.at[1], 3, chunk)
+                if chunk == QD_CHUNKS // 2 - 1:
+                    back_dkv(0, 0, 1, guest).start()
+
+        @pl.when(has_next & ~is_early)
+        def _():
+            all_queries(late)
 
 
         @pl.when(gst == 0)
         def _():
-            finish_dkv(0, 0)
+            @pl.when(~is_early)
+            def _():
+                finish_dkv(0, 0)
+                back_dkv(0, 0, 1, guest).start()
+
             finish_dkv(0, 1)
 
         for part in range(2):
@@ -590,7 +619,6 @@
             @pl.when(gst == 0)
             def _():
                 if part == 0:
-                    back_dkv(0, 0, 1, guest).start()
                     back_dkv(0, 1, 1, guest).start()
                 back_dkv(1, part, 3, host(pair)).start()
 
@@ -623,7 +651,8 @@
             back_dkv(gst, part, 1, guest).wait_send()
             back_dkv(res, part, 3, host(pair)).wait_send()
             back_dkv(0, part, 1, guest).wait_recv()
-        back_dq().wait_recv()
+        back_dq(0).wait_recv()
+        back_dq(1).wait_recv()
 
 
 def store_kernel(dq_in, dkv_in, dq_hbm, dk_hbm, dv_hbm, sem):
@@ -660,7 +689,7 @@
                 pltpu.VMEM((2, head, flat), full), pltpu.VMEM((2, rows, head), full), pltpu.VMEM((2, rows, head), full),
                 pltpu.VMEM((2, flat, head), low), pltpu.VMEM((2, 2, rows, head), low),
                 dma((7,)), dma((moves,)), dma((moves,)), dma((2, moves)), dma((2, moves)),
-                dma((3, KV_CHUNKS)), dma((3, KV_CHUNKS)), dma((3, QD_CHUNKS + 1)), dma((3, QD_CHUNKS + 1)), dma((QD_CHUNKS + 1,)), dma((5,)), dma((3,)),
+                dma((3, KV_CHUNKS)), dma((3, KV_CHUNKS)), dma((3, QD_CHUNKS + 1)), dma((3, QD_CHUNKS + 1)), dma((QD_CHUNKS + 1,)), dma((6,)), dma((4,)),
             ],
             compiler_params=pltpu.CompilerParams(collective_id=0, has_side_effects=True),
         )(queries.reshape(flat, head), keys, values, attn_out.reshape(flat, head), d_out.reshape(flat, head),

time: 35.2 us -> 34 us (0.966)
  Pallas kernels: 34.3 us -> 33.1 us
    pallas_call x1, Pallas kernels: 33.5 us -> 32.3 us  [local(): pl.pallas_call(functools.partial(backward_kernel, (outer, inner, rows, he...]
where the time goes in v6:
time: 34 us; the launch traced here: 33.9 us
  Pallas kernels  33.1 us (97%)
  between operations  0.82 us (2%)
    pallas_call x1, Pallas kernels, local(): pl.pallas_call(functools.partial(backward_kernel, (outer, inner, rows, he...  32.3 us
    pallas_call x1, Pallas kernels, local(): pl.pallas_call(store_kernel, out_shape=(jax.ShapeDtypeStruct((flat, head)...  0.81 us

profile of v6, /device:TPU:123, one launch (start us, length us, event | category | flops | bytes accessed | tf_op | source)
XLA Modules:
  0.0 33.9 jit_solution(4217782412486067094)
XLA Ops:
  0.6 32.3 %shard_map.94 = (bf16[1024,128]{1,0:T(8,128)(2,1)S(1)}, bf16[2,512,128]{2,1,0:T(8,128)(2,1)S(1)}) custom-call(bf16[1024,128]{1,0:T(8,128)(2,1)} %bitcast.6, bf16[512,128]{1,0:T(8,128)(2,1)} %k_hbm.1, bf16[512,128]{1,0:T(8,128)(2,1)} %v_hbm.1, bf16[1024,128]{1,0:T(8,128)(2,1)} %bitcast.7, bf16[1024,128]{1,0:T(8,128)(2,1)} %bitcast.8, f32[2,512]{1,0:T(2,128)} %bitcast.9, ...), custom_call_target="tpu_custom_call" | custom-call | tf_op jit(solution)/shard_map/pallas_call | solution.py:678
  32.9 0.8 %shard_map.95 = (bf16[1024,128]{1,0:T(8,128)(2,1)}, bf16[512,128]{1,0:T(8,128)(2,1)}, bf16[512,128]{1,0:T(8,128)(2,1)}) custom-call(bf16[1024,128]{1,0:T(8,128)(2,1)S(1)} %get-tuple-element.8.dq_in, bf16[2,512,128]{2,1,0:T(8,128)(2,1)S(1)} %get-tuple-element.9.dkv_in), custom_call_target="tpu_custom_call" | custom-call | tf_op jit(solution)/shard_map/pallas_call | solution.py:697

commit v7 on v6

--- a/solution.py
+++ b/solution.py
@@ -91,7 +91,7 @@
         (is_host, guest), (is_helper, host(pair)), (is_helper, my_host), (is_helper, (my_host + inner) % group), (is_host, helper(pair)),
         (is_host & has_prev & ~past_cut, host(pair - 1)), (is_host & has_prev2 & ~past_cut & ~past_cut2, host(pair - 2)),
         (is_helper & has_next & ~at_cut, host(pair + 1)), (is_helper & has_next2 & ~at_cut & ~before_cut, host(pair + 2)),
-        (is_carrier, host(half - 2)), (is_host & (past_cut | past_cut2), visitor(half - 1)),
+        (is_host & past_cut, helper(half - 2)), (is_host & (past_cut | past_cut2), visitor(half - 1)),
         (is_helper & at_cut, visitor(half)), (is_helper & at_cut, visitor(half + 1)),
         (is_helper & before_cut, visitor(half)),
     ):
@@ -103,7 +103,7 @@
     for known, count in (
         (is_host & has_next & ~at_cut, 1), (is_host & has_next2 & ~at_cut & ~before_cut, 1),
         (is_host & has_prev & ~past_cut, 1), (is_host & has_prev2 & ~past_cut & ~past_cut2, 1),
-        (is_host & before_cut, 1), (is_carrier, 2), (goes_left1, 2), (goes_left2, 1),
+        (is_helper & before_cut, 1), (is_carrier, 2), (goes_left1, 2), (goes_left2, 1),
     ):
         arrivals = arrivals + jnp.where(known, count, 0)
     for load in loads:
@@ -152,8 +152,7 @@
 
     def right2(chunk):
         part = kv_rows(chunk)
-        to = jnp.where(before_cut, visitor(half - 1), host(pair + 2))
-        return remote(kv_s.at[1, :, part], kv_w.at[2, :, part], right_send.at[2, chunk], right_recv.at[2, chunk], to)
+        return remote(kv_s.at[1, :, part], kv_w.at[2, :, part], right_send.at[2, chunk], right_recv.at[2, chunk], host(pair + 2))
 
     def carry1(slot, chunk):
         part = kv_rows(chunk)
@@ -218,7 +217,7 @@
                 item().start()
 
     sends_right1 = is_host & has_next
-    sends_right2 = is_host & has_next2 & (res == 1) & ~at_cut
+    sends_right2 = is_host & has_next2 & (res == 1) & ~at_cut & ~before_cut
     sends_left1 = is_host & has_prev & ~past_cut
     sends_left2 = is_host & has_prev2 & (res == 0) & ~past_cut & ~past_cut2
     waits_left2 = (pair // half) % 2 == res
@@ -367,7 +366,7 @@
 
         for chunk in range(QD_CHUNKS):
             guest_qd(chunk).wait_recv()
-            when(relays_left1 & has_next, lambda: left1(gst, chunk))
+            when(relays_left1, lambda: left1(gst, chunk))
             fwd_qd(gst, chunk).start()
             when(relays_left2 & ~waits_left2, lambda: left2(chunk))
             if chunk >= QD_CHUNKS // 2:
@@ -382,17 +381,12 @@
                     early_keys()
                 early_tiles(chunk)
 
-        for chunk in range(QD_CHUNKS // 2):
-            when(relays_left1 & ~has_next, lambda: left1(gst, chunk))
         @pl.when(past_cut)
         def _():
             early_keys()
 
-            def both(chunk, _):
-                early_tiles(chunk)
-                return 0
-
-            lax.fori_loop(0, QD_CHUNKS, both, 0)
+            for chunk in range(QD_CHUNKS):
+                q_tile(kv_w.at[soon], 2, 0, rows, prev_off, gst, chunk)
 
         for chunk in range(QD_CHUNKS // 2, QD_CHUNKS):
             when(relays_left2 & waits_left2, lambda: left2(chunk))
@@ -407,9 +401,6 @@
         @pl.when(has_prev2 & ~past_cut)
         def _():
             far_keys()
-
-        for chunk in range(QD_CHUNKS // 2, QD_CHUNKS):
-            when(relays_left1 & ~has_next, lambda: left1(gst, chunk))
 
         def late_keys(slot, part, step):
             @pl.when(has_prev)
@@ -438,6 +429,9 @@
 
         @pl.when(past_cut)
         def _():
+            key_t[2] = kv_w[soon, 0, :, :].T
+            for chunk in range(QD_CHUNKS):
+                q_tile(kv_w.at[soon], 2, 0, rows, prev_off, res, chunk)
             far_keys()
 
         finish_dq(res, dq_out, 0)
@@ -510,13 +504,13 @@
         carry(0)
         for chunk in range(KV_CHUNKS):
             fwd_kv(res, chunk).wait_recv()
+        when(before_cut, *[lambda chunk=chunk: right2(chunk) for chunk in range(KV_CHUNKS)])
         fwd_ld(res).wait_recv()
         for chunk in range(QD_CHUNKS):
             fwd_qd(res, chunk).wait_recv()
             diagonal(res, chunk)
         for chunk in range(QD_CHUNKS):
             when(past_cut | at_cut, lambda: guest_qd(chunk))
-        carry(2)
         for chunk in range(KV_CHUNKS):
             fwd_kv(gst, chunk).wait_recv()
         fwd_ld(gst).wait_recv()
@@ -630,10 +624,15 @@
                 relay_qd1(chunk).wait_send()
                 relay_qd(chunk).wait_send()
 
+        @pl.when(before_cut)
+        def _():
+            for chunk in range(KV_CHUNKS):
+                right2(chunk).wait_send()
+
         @pl.when(is_carrier)
         def _():
             for chunk in range(KV_CHUNKS):
-                for slot in range(3):
+                for slot in range(2):
                     carry1(slot, chunk).wait_send()
                 carry2(chunk).wait_send()
 

time: 34 us -> 33.7 us (level)
  the two profiles are of different devices: /device:TPU:123 before, /device:TPU:3 now
where the time goes in v7:
time: 33.7 us; the launch traced here: 33.6 us
  Pallas kernels  32.8 us (97%)
  between operations  0.8 us (2%)
    pallas_call x1, Pallas kernels, local(): pl.pallas_call(functools.partial(backward_kernel, (outer, inner, rows, he...  32 us
    pallas_call x1, Pallas kernels, local(): pl.pallas_call(store_kernel, out_shape=(jax.ShapeDtypeStruct((flat, head)...  0.81 us

profile of v7, /device:TPU:3, one launch (start us, length us, event | category | flops | bytes accessed | tf_op | source)
XLA Modules:
  0.0 33.6 jit_solution(2545691270795887814)
XLA Ops:
  0.6 32.0 %shard_map.94 = (bf16[1024,128]{1,0:T(8,128)(2,1)S(1)}, bf16[2,512,128]{2,1,0:T(8,128)(2,1)S(1)}) custom-call(bf16[1024,128]{1,0:T(8,128)(2,1)} %bitcast.6, bf16[512,128]{1,0:T(8,128)(2,1)} %k_hbm.1, bf16[512,128]{1,0:T(8,128)(2,1)} %v_hbm.1, bf16[1024,128]{1,0:T(8,128)(2,1)} %bitcast.7, bf16[1024,128]{1,0:T(8,128)(2,1)} %bitcast.8, f32[2,512]{1,0:T(2,128)} %bitcast.9, ...), custom_call_target="tpu_custom_call" | custom-call | tf_op jit(solution)/shard_map/pallas_call | solution.py:677
  32.6 0.8 %shard_map.95 = (bf16[1024,128]{1,0:T(8,128)(2,1)}, bf16[512,128]{1,0:T(8,128)(2,1)}, bf16[512,128]{1,0:T(8,128)(2,1)}) custom-call(bf16[1024,128]{1,0:T(8,128)(2,1)S(1)} %get-tuple-element.8.dq_in, bf16[2,512,128]{2,1,0:T(8,128)(2,1)S(1)} %get-tuple-element.9.dkv_in), custom_call_target="tpu_custom_call" | custom-call | tf_op jit(solution)/shard_map/pallas_call | solution.py:696

commit v8 on v7

--- a/solution.py
+++ b/solution.py
@@ -402,8 +402,8 @@
         def _():
             far_keys()
 
-        def late_keys(slot, part, step):
-            @pl.when(has_prev)
+        def late_keys(slot, part, step, cond=True):
+            @pl.when(has_prev & cond)
             def _():
                 for index in range(2):
                     q_tile(kv_w.at[1 - soon], 2, part * k_part, (part + 1) * k_part, late_off, slot, 2 * step + index)
@@ -422,13 +422,15 @@
             if last:
                 back_dq(0).start()
                 finish_dq(gst, dq_fin.at[gst], 1)
-            late_keys(res, chunk, 0)
+            late_keys(res, chunk, 0, last | ~past_cut)
             if last:
                 back_dq(1).start()
-            late_keys(res, chunk, 1)
+            late_keys(res, chunk, 1, last | ~past_cut)
 
         @pl.when(past_cut)
         def _():
+            late_keys(res, 0, 0)
+            late_keys(res, 0, 1)
             key_t[2] = kv_w[soon, 0, :, :].T
             for chunk in range(QD_CHUNKS):
                 q_tile(kv_w.at[soon], 2, 0, rows, prev_off, res, chunk)

time: 33.7 us -> 33.7 us (level)
  no operation moved by 1% of the time
where the time goes in v8:
time: 33.7 us; the launch traced here: 33.6 us
  Pallas kernels  32.8 us (97%)
  between operations  0.8 us (2%)
    pallas_call x1, Pallas kernels, local(): pl.pallas_call(functools.partial(backward_kernel, (outer, inner, rows, he...  32 us
    pallas_call x1, Pallas kernels, local(): pl.pallas_call(store_kernel, out_shape=(jax.ShapeDtypeStruct((flat, head)...  0.81 us

profile of v8, /device:TPU:3, one launch (start us, length us, event | category | flops | bytes accessed | tf_op | source)
XLA Modules:
  0.0 33.6 jit_solution(18189895902008344197)
XLA Ops:
  0.6 32.0 %shard_map.94 = (bf16[1024,128]{1,0:T(8,128)(2,1)S(1)}, bf16[2,512,128]{2,1,0:T(8,128)(2,1)S(1)}) custom-call(bf16[1024,128]{1,0:T(8,128)(2,1)} %bitcast.6, bf16[512,128]{1,0:T(8,128)(2,1)} %k_hbm.1, bf16[512,128]{1,0:T(8,128)(2,1)} %v_hbm.1, bf16[1024,128]{1,0:T(8,128)(2,1)} %bitcast.7, bf16[1024,128]{1,0:T(8,128)(2,1)} %bitcast.8, f32[2,512]{1,0:T(2,128)} %bitcast.9, ...), custom_call_target="tpu_custom_call" | custom-call | tf_op jit(solution)/shard_map/pallas_call | solution.py:679
  32.6 0.8 %shard_map.95 = (bf16[1024,128]{1,0:T(8,128)(2,1)}, bf16[512,128]{1,0:T(8,128)(2,1)}, bf16[512,128]{1,0:T(8,128)(2,1)}) custom-call(bf16[1024,128]{1,0:T(8,128)(2,1)S(1)} %get-tuple-element.8.dq_in, bf16[2,512,128]{2,1,0:T(8,128)(2,1)S(1)} %get-tuple-element.9.dkv_in), custom_call_target="tpu_custom_call" | custom-call | tf_op jit(solution)/shard_map/pallas_call | solution.py:698
